TPU v7x, 32 devices: a whole 2x2x4 slice. The times are simulated.
32 devices in a mesh: tm: 16 (over z, y, x), space: 2 (over core).
Axes of the slice: x: 2, y: 2, z: 4, core: 2. Of those that a mesh axis runs over, the one named last changes fastest.
Arguments:
- forcing: float32 [16, 64, 64, 256], P('tm', None, None, 'space'), may hold values from -6 to 6
- initial: float32 [64, 64, 256], P('tm', None, 'space'), may hold values from -6 to 6
- diffusion: float32 [64, 64, 256], P('tm', None, 'space'), may hold values from 0.25 to 4
- drift: float32 [64, 64, 256], P('tm', None, 'space'), may hold values from 0.2 to 1.5
Outputs:
- states: float32 [16, 64, 64, 256], P('tm', None, None, 'space')
All inputs are finite; a program needn't handle non-finite values.
Results may differ from a plain program's by a relative error of at most 0.00002.
Values sent between devices are 32-bit elements; how exact they have to be, the bound alone decides.
No kernel may reach another device: no remote copies, remote signals or barrier semaphores. Data moves between devices by JAX's collectives and lax.ppermute only.
A program may use at most 64 MiB of HBM per device.

v0:
```python
import jax
import jax.numpy as jnp
from jax import lax
from jax.sharding import PartitionSpec as P

NT = 16


def padded(shard, sides, width):
    for axis, dim in sides:
        size, length = (lax.axis_size(axis), shard.shape[dim])
        up = [(i, (i + 1) % size) for i in range(size - 1)]
        down = [(j, i) for i, j in up]
        last = lax.slice_in_dim(shard, length - width, length, axis=dim)
        leading = lax.slice_in_dim(shard, 0, width, axis=dim)
        before = lax.ppermute(last, axis, up)
        after = lax.ppermute(leading, axis, down)
        shard = jnp.concatenate([before, shard, after], axis=dim)
    return shard


def relax_cells(field, source, diffus, drift_rate):
    widened = jnp.pad(field, ((0, 0), (1, 1), (0, 0)))
    beside = field[2:, :, 1:-1] + field[:-2, :, 1:-1]
    beside = beside + field[1:-1, :, 2:] + field[1:-1, :, :-2]
    beside = beside + widened[1:-1, 2:, 1:-1] + widened[1:-1, :-2, 1:-1]
    upstream = field[:-2, :, 1:-1]
    return (source + diffus * beside + drift_rate * upstream) / (1.0 + 6.0 * diffus + drift_rate)


def trim_rim(values, margin_cut):
    zlen = values.shape[-3]
    ylen = values.shape[-1]
    return values[..., margin_cut : zlen - margin_cut, :, margin_cut : ylen - margin_cut]


def sweep_block(widened, coef_wide, depth):
    grown = widened[0]
    for inner in range(depth):
        margin_cut = inner + 1
        grown = relax_cells(
            grown,
            trim_rim(widened[1], margin_cut),
            trim_rim(coef_wide[0], margin_cut),
            trim_rim(coef_wide[1], margin_cut),
        )
    return grown


def per_device(forcing, initial, diffusion, drift):
    xparts = lax.axis_size("tm") // NT
    slabs = lax.all_to_all(forcing, "tm", split_axis=1, concat_axis=0, tiled=True)
    zcells = slabs.shape[1]
    xpart = slabs.shape[2]
    ycells = slabs.shape[3]
    slabs = slabs.reshape(NT, xparts, zcells, xpart, ycells).transpose(0, 2, 1, 3, 4)
    slabs = slabs.reshape(NT, zcells, xparts * xpart, ycells)
    coeffs = jnp.stack((diffusion, drift))
    coef_wide = padded(coeffs, (("tm", 1), ("space", 3)), 4)

    def advance(current, forcing_now):
        source = current + forcing_now
        field = current
        widened = padded(jnp.stack((field, source)), (("tm", 1), ("space", 3)), 4)
        field = sweep_block(widened, coef_wide, 4)
        return (field, field)

    final, result = lax.scan(advance, initial, slabs)
    result = result.reshape(NT, zcells, xparts, xpart, ycells).transpose(0, 2, 1, 3, 4)
    result = result.reshape(NT * xparts, zcells, xpart, ycells)
    return lax.all_to_all(result, "tm", split_axis=0, concat_axis=1, tiled=True)


def solution(mesh):
    in_specs = (
        P("tm", None, None, "space"),
        P("tm", None, "space"),
        P("tm", None, "space"),
        P("tm", None, "space"),
    )
    out_specs = P("tm", None, None, "space")
    return jax.shard_map(
        per_device, mesh=mesh, in_specs=in_specs, out_specs=out_specs, check_vma=False
    )
```

profile of v0, /device:TPU:0, one launch (start us, length us, event | category | flops | bytes accessed | tf_op | source)
XLA Modules:
  0.0 733.7 jit_solution(16396993088721520868)
XLA Ops:
  14.0 12.1 %collective-permute-done.4 = f32[2,4,64,128]{2,3,1,0:T(8,128)S(1)} collective-permute-done((f32[2,4,64,128]{2,3,1,0:T(8,128)S(1)}, f32[2,4,64,128]{2,3,1,0:T(8,128)S(1)}, u32[]{:S(2)}, u32[]{:S(2)}) %collective-permute-start.4) | collective-permute-done | bytes 262176 | tf_op jit(solution)/shard_map/ppermute | solution.py:16
  26.1 33.1 %collective-permute-done.5 = f32[2,4,64,128]{2,3,1,0:T(8,128)S(1)} collective-permute-done((f32[2,4,64,128]{2,3,1,0:T(8,128)S(1)}, f32[2,4,64,128]{2,3,1,0:T(8,128)S(1)}, u32[]{:S(2)}, u32[]{:S(2)}) %collective-permute-start.5) | collective-permute-done | bytes 262176 | tf_op jit(solution)/shard_map/ppermute | solution.py:17
  65.0 608.6 %while.14 = (s32[]{:T(128)}, f32[4,64,128]{1,2,0:T(8,128)S(1)}, f32[16,4,64,128]{3,2,1,0:T(8,128)}, f32[16,4,64,128]{3,2,1,0:T(8,128)}, f32[2,12,64,136]{2,3,1,0:T(8,128)}, /*index=5*/s32[]{:T(128)}) while((s32[]{:T(128)}, f32[4,64,128]{1,2,0:T(8,128)S(1)}, f32[16,4,64,128]{3,2,1,0:T(8,128)}, f32[16,4,64,128]{3,2,1,0:T(8,128)}, ...), condition=%wide.region_1.2_spmd, body=%wide.region_0.1_spmd.sunk | while | flops 4248066 | bytes 30435600 | solution.py:68
  72.2 10.8 %collective-permute-done = f32[2,4,64,128]{2,3,1,0:T(8,128)S(1)} collective-permute-done((f32[2,4,64,128]{2,3,1,0:T(8,128)S(1)}, f32[2,4,64,128]{2,3,1,0:T(8,128)S(1)}, u32[]{:S(2)}, u32[]{:S(2)}) %collective-permute-start) | collective-permute-done | bytes 262176 | tf_op jit(solution)/shard_map/while/body/eval_jaxpr/ppermute | solution.py:17
  109.7 10.8 %collective-permute-done = f32[2,4,64,128]{2,3,1,0:T(8,128)S(1)} collective-permute-done((f32[2,4,64,128]{2,3,1,0:T(8,128)S(1)}, f32[2,4,64,128]{2,3,1,0:T(8,128)S(1)}, u32[]{:S(2)}, u32[]{:S(2)}) %collective-permute-start) | collective-permute-done | bytes 262176 | tf_op jit(solution)/shard_map/while/body/eval_jaxpr/ppermute | solution.py:17
  120.5 11.4 %collective-permute-done.1 = f32[2,4,64,128]{2,3,1,0:T(8,128)S(1)} collective-permute-done((f32[2,4,64,128]{2,3,1,0:T(8,128)S(1)}, f32[2,4,64,128]{2,3,1,0:T(8,128)S(1)}, u32[]{:S(2)}, u32[]{:S(2)}) %collective-permute-start.1) | collective-permute-done | bytes 262176 | tf_op jit(solution)/shard_map/while/body/eval_jaxpr/ppermute | solution.py:16
  148.0 10.8 %collective-permute-done = f32[2,4,64,128]{2,3,1,0:T(8,128)S(1)} collective-permute-done((f32[2,4,64,128]{2,3,1,0:T(8,128)S(1)}, f32[2,4,64,128]{2,3,1,0:T(8,128)S(1)}, u32[]{:S(2)}, u32[]{:S(2)}) %collective-permute-start) | collective-permute-done | bytes 262176 | tf_op jit(solution)/shard_map/while/body/eval_jaxpr/ppermute | solution.py:17
  185.8 10.8 %collective-permute-done = f32[2,4,64,128]{2,3,1,0:T(8,128)S(1)} collective-permute-done((f32[2,4,64,128]{2,3,1,0:T(8,128)S(1)}, f32[2,4,64,128]{2,3,1,0:T(8,128)S(1)}, u32[]{:S(2)}, u32[]{:S(2)}) %collective-permute-start) | collective-permute-done | bytes 262176 | tf_op jit(solution)/shard_map/while/body/eval_jaxpr/ppermute | solution.py:17
  196.6 11.4 %collective-permute-done.1 = f32[2,4,64,128]{2,3,1,0:T(8,128)S(1)} collective-permute-done((f32[2,4,64,128]{2,3,1,0:T(8,128)S(1)}, f32[2,4,64,128]{2,3,1,0:T(8,128)S(1)}, u32[]{:S(2)}, u32[]{:S(2)}) %collective-permute-start.1) | collective-permute-done | bytes 262176 | tf_op jit(solution)/shard_map/while/body/eval_jaxpr/ppermute | solution.py:16
  224.2 10.8 %collective-permute-done = f32[2,4,64,128]{2,3,1,0:T(8,128)S(1)} collective-permute-done((f32[2,4,64,128]{2,3,1,0:T(8,128)S(1)}, f32[2,4,64,128]{2,3,1,0:T(8,128)S(1)}, u32[]{:S(2)}, u32[]{:S(2)}) %collective-permute-start) | collective-permute-done | bytes 262176 | tf_op jit(solution)/shard_map/while/body/eval_jaxpr/ppermute | solution.py:17
  262.0 10.8 %collective-permute-done = f32[2,4,64,128]{2,3,1,0:T(8,128)S(1)} collective-permute-done((f32[2,4,64,128]{2,3,1,0:T(8,128)S(1)}, f32[2,4,64,128]{2,3,1,0:T(8,128)S(1)}, u32[]{:S(2)}, u32[]{:S(2)}) %collective-permute-start) | collective-permute-done | bytes 262176 | tf_op jit(solution)/shard_map/while/body/eval_jaxpr/ppermute | solution.py:17
  272.8 11.4 %collective-permute-done.1 = f32[2,4,64,128]{2,3,1,0:T(8,128)S(1)} collective-permute-done((f32[2,4,64,128]{2,3,1,0:T(8,128)S(1)}, f32[2,4,64,128]{2,3,1,0:T(8,128)S(1)}, u32[]{:S(2)}, u32[]{:S(2)}) %collective-permute-start.1) | collective-permute-done | bytes 262176 | tf_op jit(solution)/shard_map/while/body/eval_jaxpr/ppermute | solution.py:16
  300.4 10.8 %collective-permute-done = f32[2,4,64,128]{2,3,1,0:T(8,128)S(1)} collective-permute-done((f32[2,4,64,128]{2,3,1,0:T(8,128)S(1)}, f32[2,4,64,128]{2,3,1,0:T(8,128)S(1)}, u32[]{:S(2)}, u32[]{:S(2)}) %collective-permute-start) | collective-permute-done | bytes 262176 | tf_op jit(solution)/shard_map/while/body/eval_jaxpr/ppermute | solution.py:17
  338.2 10.8 %collective-permute-done = f32[2,4,64,128]{2,3,1,0:T(8,128)S(1)} collective-permute-done((f32[2,4,64,128]{2,3,1,0:T(8,128)S(1)}, f32[2,4,64,128]{2,3,1,0:T(8,128)S(1)}, u32[]{:S(2)}, u32[]{:S(2)}) %collective-permute-start) | collective-permute-done | bytes 262176 | tf_op jit(solution)/shard_map/while/body/eval_jaxpr/ppermute | solution.py:17
  349.0 11.4 %collective-permute-done.1 = f32[2,4,64,128]{2,3,1,0:T(8,128)S(1)} collective-permute-done((f32[2,4,64,128]{2,3,1,0:T(8,128)S(1)}, f32[2,4,64,128]{2,3,1,0:T(8,128)S(1)}, u32[]{:S(2)}, u32[]{:S(2)}) %collective-permute-start.1) | collective-permute-done | bytes 262176 | tf_op jit(solution)/shard_map/while/body/eval_jaxpr/ppermute | solution.py:16
  376.6 10.8 %collective-permute-done = f32[2,4,64,128]{2,3,1,0:T(8,128)S(1)} collective-permute-done((f32[2,4,64,128]{2,3,1,0:T(8,128)S(1)}, f32[2,4,64,128]{2,3,1,0:T(8,128)S(1)}, u32[]{:S(2)}, u32[]{:S(2)}) %collective-permute-start) | collective-permute-done | bytes 262176 | tf_op jit(solution)/shard_map/while/body/eval_jaxpr/ppermute | solution.py:17
  414.3 10.8 %collective-permute-done = f32[2,4,64,128]{2,3,1,0:T(8,128)S(1)} collective-permute-done((f32[2,4,64,128]{2,3,1,0:T(8,128)S(1)}, f32[2,4,64,128]{2,3,1,0:T(8,128)S(1)}, u32[]{:S(2)}, u32[]{:S(2)}) %collective-permute-start) | collective-permute-done | bytes 262176 | tf_op jit(solution)/shard_map/while/body/eval_jaxpr/ppermute | solution.py:17
  425.1 11.4 %collective-permute-done.1 = f32[2,4,64,128]{2,3,1,0:T(8,128)S(1)} collective-permute-done((f32[2,4,64,128]{2,3,1,0:T(8,128)S(1)}, f32[2,4,64,128]{2,3,1,0:T(8,128)S(1)}, u32[]{:S(2)}, u32[]{:S(2)}) %collective-permute-start.1) | collective-permute-done | bytes 262176 | tf_op jit(solution)/shard_map/while/body/eval_jaxpr/ppermute | solution.py:16
  452.7 10.8 %collective-permute-done = f32[2,4,64,128]{2,3,1,0:T(8,128)S(1)} collective-permute-done((f32[2,4,64,128]{2,3,1,0:T(8,128)S(1)}, f32[2,4,64,128]{2,3,1,0:T(8,128)S(1)}, u32[]{:S(2)}, u32[]{:S(2)}) %collective-permute-start) | collective-permute-done | bytes 262176 | tf_op jit(solution)/shard_map/while/body/eval_jaxpr/ppermute | solution.py:17
  501.3 11.4 %collective-permute-done.1 = f32[2,4,64,128]{2,3,1,0:T(8,128)S(1)} collective-permute-done((f32[2,4,64,128]{2,3,1,0:T(8,128)S(1)}, f32[2,4,64,128]{2,3,1,0:T(8,128)S(1)}, u32[]{:S(2)}, u32[]{:S(2)}) %collective-permute-start.1) | collective-permute-done | bytes 262176 | tf_op jit(solution)/shard_map/while/body/eval_jaxpr/ppermute | solution.py:16
  528.9 10.8 %collective-permute-done = f32[2,4,64,128]{2,3,1,0:T(8,128)S(1)} collective-permute-done((f32[2,4,64,128]{2,3,1,0:T(8,128)S(1)}, f32[2,4,64,128]{2,3,1,0:T(8,128)S(1)}, u32[]{:S(2)}, u32[]{:S(2)}) %collective-permute-start) | collective-permute-done | bytes 262176 | tf_op jit(solution)/shard_map/while/body/eval_jaxpr/ppermute | solution.py:17
  577.5 11.4 %collective-permute-done.1 = f32[2,4,64,128]{2,3,1,0:T(8,128)S(1)} collective-permute-done((f32[2,4,64,128]{2,3,1,0:T(8,128)S(1)}, f32[2,4,64,128]{2,3,1,0:T(8,128)S(1)}, u32[]{:S(2)}, u32[]{:S(2)}) %collective-permute-start.1) | collective-permute-done | bytes 262176 | tf_op jit(solution)/shard_map/while/body/eval_jaxpr/ppermute | solution.py:16
  653.6 11.4 %collective-permute-done.1 = f32[2,4,64,128]{2,3,1,0:T(8,128)S(1)} collective-permute-done((f32[2,4,64,128]{2,3,1,0:T(8,128)S(1)}, f32[2,4,64,128]{2,3,1,0:T(8,128)S(1)}, u32[]{:S(2)}, u32[]{:S(2)}) %collective-permute-start.1) | collective-permute-done | bytes 262176 | tf_op jit(solution)/shard_map/while/body/eval_jaxpr/ppermute | solution.py:16
  673.6 58.7 %all_to_all.24 = f32[16,4,64,128]{3,2,1,0:T(8,128)S(1)} all-to-all(f32[16,4,64,128]{3,2,1,0:T(8,128)} %get-tuple-element.70), channel_id=1, replica_groups=mesh['tm'=16,'space'=2] {'tm'}, dimensions={0} | all-to-all | bytes 4194304 | tf_op jit(solution)/shard_map/all_to_all | solution.py:71
  (386 shorter events, 407.0 us)
Async XLA Ops:
  0.0 65.0 %all-to-all-start = ((f32[1,64,64,128]{3,2,0,1:T(8,128)}), f32[1,64,64,128]{3,2,0,1:T(8,128)}, u32[]{:S(2)}, u32[]{:S(2)}) async-start(f32[1,64,64,128]{3,2,0,1:T(8,128)} %bitcast.44), calls=%async_computation | async-start | bytes 4194304 | tf_op jit(solution)/shard_map/all_to_all | solution.py:52
  12.7 46.5 %collective-permute-start.5 = (f32[2,4,64,128]{2,3,1,0:T(8,128)S(1)}, f32[2,4,64,128]{2,3,1,0:T(8,128)S(1)}, u32[]{:S(2)}, u32[]{:S(2)}) collective-permute-start(f32[2,4,64,128]{2,3,1,0:T(8,128)S(1)} %pad_maximum_fusion.7), channel_id=1, source_target_pairs={{2,0},{4,2},{6,4},{8,6},{10,8},{12,10},{14,12},{16,14},{18,16},{20... | collective-permute-start | bytes 786440 | tf_op jit(solution)/shard_map/ppermute | solution.py:17
  67.6 25.8 %collective-permute-start.1 = (f32[2,4,64,128]{2,3,1,0:T(8,128)S(1)}, f32[2,4,64,128]{2,3,1,0:T(8,128)S(1)}, u32[]{:S(2)}, u32[]{:S(2)}) collective-permute-start(f32[2,4,64,128]{2,3,1,0:T(8,128)S(1)} %pad_maximum_fusion.15), channel_id=1, source_target_pairs={{0,2},{2,4},{4,6},{6,8},{8,10},{10,12},{12,14},{14,16},{16,18},{18... | collective-permute-start | bytes 786440 | tf_op jit(solution)/shard_map/while/body/eval_jaxpr/ppermute | solution.py:16
  103.2 17.3 %collective-permute-start = (f32[2,4,64,128]{2,3,1,0:T(8,128)S(1)}, f32[2,4,64,128]{2,3,1,0:T(8,128)S(1)}, u32[]{:S(2)}, u32[]{:S(2)}) collective-permute-start(f32[2,4,64,128]{2,3,1,0:T(8,128)S(1)} %pad_maximum_fusion.15), channel_id=1, source_target_pairs={{2,0},{4,2},{6,4},{8,6},{10,8},{12,10},{14,12},{16,14},{18,16},{20... | collective-permute-start | bytes 786440 | tf_op jit(solution)/shard_map/while/body/eval_jaxpr/ppermute | solution.py:17
  104.6 27.2 %collective-permute-start.1 = (f32[2,4,64,128]{2,3,1,0:T(8,128)S(1)}, f32[2,4,64,128]{2,3,1,0:T(8,128)S(1)}, u32[]{:S(2)}, u32[]{:S(2)}) collective-permute-start(f32[2,4,64,128]{2,3,1,0:T(8,128)S(1)} %pad_maximum_fusion.15), channel_id=1, source_target_pairs={{0,2},{2,4},{4,6},{6,8},{8,10},{10,12},{12,14},{14,16},{16,18},{18... | collective-permute-start | bytes 786440 | tf_op jit(solution)/shard_map/while/body/eval_jaxpr/ppermute | solution.py:16
  141.6 17.3 %collective-permute-start = (f32[2,4,64,128]{2,3,1,0:T(8,128)S(1)}, f32[2,4,64,128]{2,3,1,0:T(8,128)S(1)}, u32[]{:S(2)}, u32[]{:S(2)}) collective-permute-start(f32[2,4,64,128]{2,3,1,0:T(8,128)S(1)} %pad_maximum_fusion.15), channel_id=1, source_target_pairs={{2,0},{4,2},{6,4},{8,6},{10,8},{12,10},{14,12},{16,14},{18,16},{20... | collective-permute-start | bytes 786440 | tf_op jit(solution)/shard_map/while/body/eval_jaxpr/ppermute | solution.py:17
  143.0 26.6 %collective-permute-start.1 = (f32[2,4,64,128]{2,3,1,0:T(8,128)S(1)}, f32[2,4,64,128]{2,3,1,0:T(8,128)S(1)}, u32[]{:S(2)}, u32[]{:S(2)}) collective-permute-start(f32[2,4,64,128]{2,3,1,0:T(8,128)S(1)} %pad_maximum_fusion.15), channel_id=1, source_target_pairs={{0,2},{2,4},{4,6},{6,8},{8,10},{10,12},{12,14},{14,16},{16,18},{18... | collective-permute-start | bytes 786440 | tf_op jit(solution)/shard_map/while/body/eval_jaxpr/ppermute | solution.py:16
  179.4 17.3 %collective-permute-start = (f32[2,4,64,128]{2,3,1,0:T(8,128)S(1)}, f32[2,4,64,128]{2,3,1,0:T(8,128)S(1)}, u32[]{:S(2)}, u32[]{:S(2)}) collective-permute-start(f32[2,4,64,128]{2,3,1,0:T(8,128)S(1)} %pad_maximum_fusion.15), channel_id=1, source_target_pairs={{2,0},{4,2},{6,4},{8,6},{10,8},{12,10},{14,12},{16,14},{18,16},{20... | collective-permute-start | bytes 786440 | tf_op jit(solution)/shard_map/while/body/eval_jaxpr/ppermute | solution.py:17
  180.8 27.2 %collective-permute-start.1 = (f32[2,4,64,128]{2,3,1,0:T(8,128)S(1)}, f32[2,4,64,128]{2,3,1,0:T(8,128)S(1)}, u32[]{:S(2)}, u32[]{:S(2)}) collective-permute-start(f32[2,4,64,128]{2,3,1,0:T(8,128)S(1)} %pad_maximum_fusion.15), channel_id=1, source_target_pairs={{0,2},{2,4},{4,6},{6,8},{8,10},{10,12},{12,14},{14,16},{16,18},{18... | collective-permute-start | bytes 786440 | tf_op jit(solution)/shard_map/while/body/eval_jaxpr/ppermute | solution.py:16
  217.8 17.3 %collective-permute-start = (f32[2,4,64,128]{2,3,1,0:T(8,128)S(1)}, f32[2,4,64,128]{2,3,1,0:T(8,128)S(1)}, u32[]{:S(2)}, u32[]{:S(2)}) collective-permute-start(f32[2,4,64,128]{2,3,1,0:T(8,128)S(1)} %pad_maximum_fusion.15), channel_id=1, source_target_pairs={{2,0},{4,2},{6,4},{8,6},{10,8},{12,10},{14,12},{16,14},{18,16},{20... | collective-permute-start | bytes 786440 | tf_op jit(solution)/shard_map/while/body/eval_jaxpr/ppermute | solution.py:17
  219.2 26.6 %collective-permute-start.1 = (f32[2,4,64,128]{2,3,1,0:T(8,128)S(1)}, f32[2,4,64,128]{2,3,1,0:T(8,128)S(1)}, u32[]{:S(2)}, u32[]{:S(2)}) collective-permute-start(f32[2,4,64,128]{2,3,1,0:T(8,128)S(1)} %pad_maximum_fusion.15), channel_id=1, source_target_pairs={{0,2},{2,4},{4,6},{6,8},{8,10},{10,12},{12,14},{14,16},{16,18},{18... | collective-permute-start | bytes 786440 | tf_op jit(solution)/shard_map/while/body/eval_jaxpr/ppermute | solution.py:16
  257.0 27.2 %collective-permute-start.1 = (f32[2,4,64,128]{2,3,1,0:T(8,128)S(1)}, f32[2,4,64,128]{2,3,1,0:T(8,128)S(1)}, u32[]{:S(2)}, u32[]{:S(2)}) collective-permute-start(f32[2,4,64,128]{2,3,1,0:T(8,128)S(1)} %pad_maximum_fusion.15), channel_id=1, source_target_pairs={{0,2},{2,4},{4,6},{6,8},{8,10},{10,12},{12,14},{14,16},{16,18},{18... | collective-permute-start | bytes 786440 | tf_op jit(solution)/shard_map/while/body/eval_jaxpr/ppermute | solution.py:16
  293.9 17.3 %collective-permute-start = (f32[2,4,64,128]{2,3,1,0:T(8,128)S(1)}, f32[2,4,64,128]{2,3,1,0:T(8,128)S(1)}, u32[]{:S(2)}, u32[]{:S(2)}) collective-permute-start(f32[2,4,64,128]{2,3,1,0:T(8,128)S(1)} %pad_maximum_fusion.15), channel_id=1, source_target_pairs={{2,0},{4,2},{6,4},{8,6},{10,8},{12,10},{14,12},{16,14},{18,16},{20... | collective-permute-start | bytes 786440 | tf_op jit(solution)/shard_map/while/body/eval_jaxpr/ppermute | solution.py:17
  295.4 26.6 %collective-permute-start.1 = (f32[2,4,64,128]{2,3,1,0:T(8,128)S(1)}, f32[2,4,64,128]{2,3,1,0:T(8,128)S(1)}, u32[]{:S(2)}, u32[]{:S(2)}) collective-permute-start(f32[2,4,64,128]{2,3,1,0:T(8,128)S(1)} %pad_maximum_fusion.15), channel_id=1, source_target_pairs={{0,2},{2,4},{4,6},{6,8},{8,10},{10,12},{12,14},{14,16},{16,18},{18... | collective-permute-start | bytes 786440 | tf_op jit(solution)/shard_map/while/body/eval_jaxpr/ppermute | solution.py:16
  331.7 17.3 %collective-permute-start = (f32[2,4,64,128]{2,3,1,0:T(8,128)S(1)}, f32[2,4,64,128]{2,3,1,0:T(8,128)S(1)}, u32[]{:S(2)}, u32[]{:S(2)}) collective-permute-start(f32[2,4,64,128]{2,3,1,0:T(8,128)S(1)} %pad_maximum_fusion.15), channel_id=1, source_target_pairs={{2,0},{4,2},{6,4},{8,6},{10,8},{12,10},{14,12},{16,14},{18,16},{20... | collective-permute-start | bytes 786440 | tf_op jit(solution)/shard_map/while/body/eval_jaxpr/ppermute | solution.py:17
  333.1 27.2 %collective-permute-start.1 = (f32[2,4,64,128]{2,3,1,0:T(8,128)S(1)}, f32[2,4,64,128]{2,3,1,0:T(8,128)S(1)}, u32[]{:S(2)}, u32[]{:S(2)}) collective-permute-start(f32[2,4,64,128]{2,3,1,0:T(8,128)S(1)} %pad_maximum_fusion.15), channel_id=1, source_target_pairs={{0,2},{2,4},{4,6},{6,8},{8,10},{10,12},{12,14},{14,16},{16,18},{18... | collective-permute-start | bytes 786440 | tf_op jit(solution)/shard_map/while/body/eval_jaxpr/ppermute | solution.py:16
  371.5 26.6 %collective-permute-start.1 = (f32[2,4,64,128]{2,3,1,0:T(8,128)S(1)}, f32[2,4,64,128]{2,3,1,0:T(8,128)S(1)}, u32[]{:S(2)}, u32[]{:S(2)}) collective-permute-start(f32[2,4,64,128]{2,3,1,0:T(8,128)S(1)} %pad_maximum_fusion.15), channel_id=1, source_target_pairs={{0,2},{2,4},{4,6},{6,8},{8,10},{10,12},{12,14},{14,16},{16,18},{18... | collective-permute-start | bytes 786440 | tf_op jit(solution)/shard_map/while/body/eval_jaxpr/ppermute | solution.py:16
  409.3 27.2 %collective-permute-start.1 = (f32[2,4,64,128]{2,3,1,0:T(8,128)S(1)}, f32[2,4,64,128]{2,3,1,0:T(8,128)S(1)}, u32[]{:S(2)}, u32[]{:S(2)}) collective-permute-start(f32[2,4,64,128]{2,3,1,0:T(8,128)S(1)} %pad_maximum_fusion.15), channel_id=1, source_target_pairs={{0,2},{2,4},{4,6},{6,8},{8,10},{10,12},{12,14},{14,16},{16,18},{18... | collective-permute-start | bytes 786440 | tf_op jit(solution)/shard_map/while/body/eval_jaxpr/ppermute | solution.py:16
  447.7 26.6 %collective-permute-start.1 = (f32[2,4,64,128]{2,3,1,0:T(8,128)S(1)}, f32[2,4,64,128]{2,3,1,0:T(8,128)S(1)}, u32[]{:S(2)}, u32[]{:S(2)}) collective-permute-start(f32[2,4,64,128]{2,3,1,0:T(8,128)S(1)} %pad_maximum_fusion.15), channel_id=1, source_target_pairs={{0,2},{2,4},{4,6},{6,8},{8,10},{10,12},{12,14},{14,16},{16,18},{18... | collective-permute-start | bytes 786440 | tf_op jit(solution)/shard_map/while/body/eval_jaxpr/ppermute | solution.py:16
  485.5 27.2 %collective-permute-start.1 = (f32[2,4,64,128]{2,3,1,0:T(8,128)S(1)}, f32[2,4,64,128]{2,3,1,0:T(8,128)S(1)}, u32[]{:S(2)}, u32[]{:S(2)}) collective-permute-start(f32[2,4,64,128]{2,3,1,0:T(8,128)S(1)} %pad_maximum_fusion.15), channel_id=1, source_target_pairs={{0,2},{2,4},{4,6},{6,8},{8,10},{10,12},{12,14},{14,16},{16,18},{18... | collective-permute-start | bytes 786440 | tf_op jit(solution)/shard_map/while/body/eval_jaxpr/ppermute | solution.py:16
  523.9 26.6 %collective-permute-start.1 = (f32[2,4,64,128]{2,3,1,0:T(8,128)S(1)}, f32[2,4,64,128]{2,3,1,0:T(8,128)S(1)}, u32[]{:S(2)}, u32[]{:S(2)}) collective-permute-start(f32[2,4,64,128]{2,3,1,0:T(8,128)S(1)} %pad_maximum_fusion.15), channel_id=1, source_target_pairs={{0,2},{2,4},{4,6},{6,8},{8,10},{10,12},{12,14},{14,16},{16,18},{18... | collective-permute-start | bytes 786440 | tf_op jit(solution)/shard_map/while/body/eval_jaxpr/ppermute | solution.py:16
  561.6 27.2 %collective-permute-start.1 = (f32[2,4,64,128]{2,3,1,0:T(8,128)S(1)}, f32[2,4,64,128]{2,3,1,0:T(8,128)S(1)}, u32[]{:S(2)}, u32[]{:S(2)}) collective-permute-start(f32[2,4,64,128]{2,3,1,0:T(8,128)S(1)} %pad_maximum_fusion.15), channel_id=1, source_target_pairs={{0,2},{2,4},{4,6},{6,8},{8,10},{10,12},{12,14},{14,16},{16,18},{18... | collective-permute-start | bytes 786440 | tf_op jit(solution)/shard_map/while/body/eval_jaxpr/ppermute | solution.py:16
  600.0 26.6 %collective-permute-start.1 = (f32[2,4,64,128]{2,3,1,0:T(8,128)S(1)}, f32[2,4,64,128]{2,3,1,0:T(8,128)S(1)}, u32[]{:S(2)}, u32[]{:S(2)}) collective-permute-start(f32[2,4,64,128]{2,3,1,0:T(8,128)S(1)} %pad_maximum_fusion.15), channel_id=1, source_target_pairs={{0,2},{2,4},{4,6},{6,8},{8,10},{10,12},{12,14},{14,16},{16,18},{18... | collective-permute-start | bytes 786440 | tf_op jit(solution)/shard_map/while/body/eval_jaxpr/ppermute | solution.py:16
  637.8 27.2 %collective-permute-start.1 = (f32[2,4,64,128]{2,3,1,0:T(8,128)S(1)}, f32[2,4,64,128]{2,3,1,0:T(8,128)S(1)}, u32[]{:S(2)}, u32[]{:S(2)}) collective-permute-start(f32[2,4,64,128]{2,3,1,0:T(8,128)S(1)} %pad_maximum_fusion.15), channel_id=1, source_target_pairs={{0,2},{2,4},{4,6},{6,8},{8,10},{10,12},{12,14},{14,16},{16,18},{18... | collective-permute-start | bytes 786440 | tf_op jit(solution)/shard_map/while/body/eval_jaxpr/ppermute | solution.py:16
  (64 other events, 923.8 us)
where the time goes:
time: 736 us; the launch traced here: 734 us
  waiting for transfers between devices  408 us (55%)
  starting transfers between devices  188 us (26%)
  blocking collectives  58.7 us (8%)
  other arithmetic  42.1 us (6%)
  local copies, waits for them, and re-layouts  34.5 us (5%)
    ppermute x34, waiting for transfers between devices, padded(): after = lax.ppermute(leading, axis, down)  208 us
    ppermute x34, waiting for transfers between devices, padded(): before = lax.ppermute(last, axis, up)  201 us
    ppermute x34, starting transfers between devices, padded(): before = lax.ppermute(last, axis, up)  134 us
    all_to_all x1, blocking collectives, per_device(): return lax.all_to_all(result, 'tm', split_axis=0, concat_axis=1, tiled=True)  58.7 us
    ppermute x34, starting transfers between devices, padded(): after = lax.ppermute(leading, axis, down)  46 us
    div x64, other arithmetic, relax_cells(): (source + diffus * beside + drift_rate * upstream) / (1.0 + 6.0 * diffus...  36.2 us
    dynamic_slice x32, local copies, waits for them, and re-layouts, per_device(): final, result = lax.scan(advance, initial, slabs)  16.7 us
  transfers between devices with their start and end apart: 69, of which 51 were waited for; matrix products, arithmetic and copies ran while one was open for 0% of the time, Pallas kernels for 0%

commit v1 on v0

--- a/solution.py
+++ b/solution.py
@@ -1,9 +1,16 @@
+import functools
+
 import jax
 import jax.numpy as jnp
 from jax import lax
+from jax.experimental import pallas as pl
+from jax.experimental.pallas import tpu as pltpu
 from jax.sharding import PartitionSpec as P
 
 NT = 16
+SWEEPS = 4
+LANES = 128
+ROWS = 8
 
 
 def padded(shard, sides, width):
@@ -47,7 +54,7 @@
     return grown
 
 
-def per_device(forcing, initial, diffusion, drift):
+def split_along_z(forcing, initial, diffusion, drift):
     xparts = lax.axis_size("tm") // NT
     slabs = lax.all_to_all(forcing, "tm", split_axis=1, concat_axis=0, tiled=True)
     zcells = slabs.shape[1]
@@ -56,19 +63,333 @@
     slabs = slabs.reshape(NT, xparts, zcells, xpart, ycells).transpose(0, 2, 1, 3, 4)
     slabs = slabs.reshape(NT, zcells, xparts * xpart, ycells)
     coeffs = jnp.stack((diffusion, drift))
-    coef_wide = padded(coeffs, (("tm", 1), ("space", 3)), 4)
+    coef_wide = padded(coeffs, (("tm", 1), ("space", 3)), SWEEPS)
 
     def advance(current, forcing_now):
         source = current + forcing_now
         field = current
-        widened = padded(jnp.stack((field, source)), (("tm", 1), ("space", 3)), 4)
-        field = sweep_block(widened, coef_wide, 4)
+        widened = padded(jnp.stack((field, source)), (("tm", 1), ("space", 3)), SWEEPS)
+        field = sweep_block(widened, coef_wide, SWEEPS)
         return (field, field)
 
     final, result = lax.scan(advance, initial, slabs)
     result = result.reshape(NT, zcells, xparts, xpart, ycells).transpose(0, 2, 1, 3, 4)
     result = result.reshape(NT * xparts, zcells, xpart, ycells)
     return lax.all_to_all(result, "tm", split_axis=0, concat_axis=1, tiled=True)
+
+
+def gray(i):
+    return i ^ (i >> 1)
+
+
+def call(kernel, out_shape, operands, flags, scratch=(), flops=0, name=None):
+    size = sum(x.size * x.dtype.itemsize for x in operands)
+    shapes = out_shape if isinstance(out_shape, (tuple, list)) else (out_shape,)
+    size += sum(functools.reduce(lambda a, b: a * b, x.shape) * 4 for x in shapes)
+    return pl.pallas_call(
+        kernel,
+        out_shape=out_shape,
+        in_specs=[pl.BlockSpec(memory_space=pltpu.SMEM)]
+        + [pl.BlockSpec(memory_space=pltpu.VMEM)] * len(operands),
+        out_specs=jax.tree.map(lambda _: pl.BlockSpec(memory_space=pltpu.VMEM), out_shape),
+        scratch_shapes=list(scratch),
+        cost_estimate=pl.CostEstimate(flops=flops or size, bytes_accessed=size, transcendentals=0),
+        name=name,
+    )(flags, *operands)
+
+
+def left_lanes():
+    return lax.broadcasted_iota(jnp.int32, (ROWS, LANES), 1) < LANES // 2
+
+
+def swap_lanes(v):
+    return pltpu.roll(v, LANES // 2, 1)
+
+
+def format_kernel(blocks, flags, raw, keep, send):
+    zrows = raw.shape[0]
+    left = left_lanes()
+
+    def body(core):
+        def step(pair, carry):
+            both = raw[pl.ds(2 * pair, 2)].reshape(LANES, LANES).T
+            for r in range(blocks):
+                low = both[2 * ROWS * r : 2 * ROWS * r + ROWS]
+                high = both[2 * ROWS * r + ROWS : 2 * ROWS * (r + 1)]
+                first = jnp.where(left, low, swap_lanes(high))
+                second = jnp.where(left, swap_lanes(low), high)
+                slot = gray(core * (blocks // 2) + r // 2) % (blocks // 2)
+                to = keep if gray(r) & 1 == core else send
+                start = slot * ROWS * zrows + 2 * pair
+                to[pl.ds(start, ROWS, stride=zrows), :] = first
+                to[pl.ds(start + 1, ROWS, stride=zrows), :] = second
+            return carry
+
+        lax.fori_loop(0, zrows // 2, step, 0)
+
+    for core in range(2):
+        pl.when(flags[1] == core)(functools.partial(body, core))
+
+
+def unformat_kernel(blocks, flags, keep, got, out):
+    zrows = out.shape[0]
+    left = left_lanes()
+
+    def body(core):
+        def step(pair, carry):
+            columns = []
+            for r in range(blocks):
+                slot = gray(core * (blocks // 2) + r // 2) % (blocks // 2)
+                src = keep if gray(r) & 1 == core else got
+                start = slot * ROWS * zrows + 2 * pair
+                first = src[pl.ds(start, ROWS, stride=zrows), :]
+                second = src[pl.ds(start + 1, ROWS, stride=zrows), :]
+                columns.append(jnp.where(left, first, swap_lanes(second)))
+                columns.append(jnp.where(left, swap_lanes(first), second))
+            both = jnp.concatenate(columns, axis=0).T
+            out[pl.ds(2 * pair, 2)] = both.reshape(2, LANES // 2, LANES)
+            return carry
+
+        lax.fori_loop(0, zrows // 2, step, 0)
+
+    for core in range(2):
+        pl.when(flags[1] == core)(functools.partial(body, core))
+
+
+def arrange_kernel(zpart, flags, got, out):
+    chips, arrays = got.shape[0], out.shape[0]
+    for k in range(arrays):
+        for chip in range(chips):
+            for upper in range(2):
+                rows = pl.ds((2 * k + upper) * zpart, zpart)
+                z = (upper * chips + chip) * zpart
+                out[k, :, pl.ds(z, zpart), :] = got[chip, :, rows, :]
+
+
+class Region:
+    def __init__(self, even):
+        self.even = even
+        left = left_lanes()[None]
+        self.left = left
+        self.other = jnp.logical_xor(left, jnp.full((1, ROWS, LANES), even, jnp.int32) == 1)
+
+    def tiles(self, plane):
+        return plane.reshape(-1, ROWS, LANES)
+
+    def plane(self, kind, m, own, core, link):
+        back = ROWS - 1 - m
+        if kind == "own":
+            v = jnp.where(self.left, self.tiles(own[m]), self.tiles(own[back]))
+        elif kind == "far":
+            c = self.tiles(core[jnp.where(self.even == 1, back, m)])
+            n = self.tiles(link[jnp.where(self.even == 1, m, back)])
+            v = jnp.where(self.other, c, n)
+        else:
+            c = self.tiles(core[jnp.where(self.even == 1, m, back)])
+            n = self.tiles(link[jnp.where(self.even == 1, back, m)])
+            v = pltpu.roll(jnp.where(self.other, n, c), LANES // 2, 2)
+        return v.reshape(-1, LANES)
+
+    def fill(self, first, own, core, link, put):
+        def run(kind, lo, hi, place):
+            def step(m, carry):
+                put(place(m), self.plane(kind, m, own, core, link))
+                return carry
+
+            if lo < hi:
+                lax.fori_loop(lo, hi, step, 0)
+
+        run("far", first, ROWS, lambda m: m)
+        run("near", 0, min(ROWS, 2 * ROWS - first), lambda m: 2 * ROWS - 1 - m)
+        run("own", 0, ROWS, lambda m: 2 * ROWS + m)
+
+
+def prep_kernel(flags, own, core, link, coef):
+    region = Region(flags[0])
+
+    def put_diffusion(i, d):
+        coef[0, i] = d
+
+    def put_drift(i, r):
+        d = coef[0, i]
+        inv = 1.0 / (1.0 + 6.0 * d + r)
+        coef[0, i] = d * inv
+        coef[1, i] = (d + r) * inv
+        coef[2, i] = inv
+
+    region.fill(0, own.at[1], core.at[1], link.at[1], put_diffusion)
+    region.fill(0, own.at[2], core.at[2], link.at[2], put_drift)
+
+
+def window_kernel(flags, own, core, link, f_own, f_core, f_link, coef, out, va, vb, c):
+    steps, planes, zrows = out.shape[0], 3 * ROWS, own.shape[1]
+    top = 2 * ROWS
+    region = Region(flags[0])
+    lane = lax.broadcasted_iota(jnp.int32, (ROWS, LANES), 1) % (LANES // 2)
+    first_x, last_x = lane == 0, lane == LANES // 2 - 1
+    inside = pl.ds(ROWS, zrows)
+    for v in (va, vb):
+        v[:, 0:ROWS] = jnp.zeros((planes + 1, ROWS, LANES), jnp.float32)
+        v[:, zrows + ROWS :] = jnp.zeros((planes + 1, ROWS, LANES), jnp.float32)
+
+    def put_field(i, plane):
+        va[i, inside] = plane
+
+    region.fill(0, own, core, link, put_field)
+    va[planes, inside] = swap_lanes(va[planes - 1, inside])
+
+    src, dst = va, vb
+    for step in range(steps):
+        current = src
+
+        def put_source(i, plane):
+            c[i] = coef[2, i] * (current[i, inside] + plane)
+
+        region.fill(SWEEPS * step + 1, f_own.at[step], f_core.at[step], f_link.at[step], put_source)
+        for sweep in range(SWEEPS):
+
+            def relax(i, carry, src=src, dst=dst):
+                for z in range(0, zrows, ROWS):
+                    at = ROWS + z
+                    v = src[i, at : at + ROWS]
+                    zm = src[i, at - 1 : at + ROWS - 1]
+                    total = src[i, at + 1 : at + ROWS + 1]
+                    total += src[i - 1, at : at + ROWS] + src[i + 1, at : at + ROWS]
+                    total += jnp.where(first_x, 0.0, pltpu.roll(v, 1, 1))
+                    total += jnp.where(last_x, 0.0, pltpu.roll(v, LANES - 1, 1))
+                    rows = slice(z, z + ROWS)
+                    dst[i, at : at + ROWS] = c[i, rows] + coef[0, i, rows] * total + coef[1, i, rows] * zm
+                return carry
+
+            lax.fori_loop(SWEEPS * step + sweep + 1, planes, relax, 0)
+            dst[planes, inside] = swap_lanes(dst[planes - 1, inside])
+            src, dst = dst, src
+        for m in range(ROWS):
+            low = src[top + m, inside].reshape(-1, ROWS, LANES)
+            high = src[planes - 1 - m, inside].reshape(-1, ROWS, LANES)
+            out[step, m] = jnp.where(region.left, low, high).reshape(-1, LANES)
+
+
+def split_along_y(forcing, initial, diffusion, drift):
+    f32 = jnp.float32
+    chips = lax.axis_size("tm") // 2
+    zpart, xlen, ylen = initial.shape
+    zlen = forcing.shape[1]
+    blocks = ylen // (2 * ROWS)
+    spw = 2 * ROWS // SWEEPS
+    t, s = lax.axis_index("tm"), lax.axis_index("space")
+    device = 2 * (t % chips) + s
+    odd = device
+    for shift in (1, 2, 4, 8):
+        odd = odd ^ (odd >> shift)
+    lower = t < chips
+    flags = jnp.stack([1 - (odd & 1), s, jnp.int32(0)]).astype(jnp.int32)
+    groups = [list(range(chips)), list(range(chips, 2 * chips))]
+    both = ("tm", "space")
+    across = []
+    for b in range(1, 2 * chips - 1, 2):
+        for base in (0, 2 * chips):
+            i, j = base + gray(b), base + gray(b + 1)
+            across += [(i, j), (j, i)]
+    hop = [(i, 2 * chips + i) for i in range(2 * chips)]
+    cores = [(0, 1), (1, 0)]
+
+    def exchange(x):
+        return lax.ppermute(x, "space", cores), lax.ppermute(x, both, across)
+
+    def to_blocks(raw):
+        zr = raw.shape[0]
+        part = jax.ShapeDtypeStruct((blocks // 2 * ROWS * zr, LANES), f32)
+        keep, send = call(
+            functools.partial(format_kernel, blocks), (part, part), (raw,), flags, name="format"
+        )
+        got = lax.ppermute(send, "space", cores)
+        whole = jnp.where(s == 0, jnp.concatenate([keep, got]), jnp.concatenate([got, keep]))
+        whole = whole.reshape(chips, ROWS, zr, LANES)
+        return lax.all_to_all(whole, "tm", 0, 0, axis_index_groups=groups, tiled=True)
+
+    fields = jnp.stack((initial, diffusion, drift))
+    far = lax.ppermute(fields, "tm", [(i, (i + chips) % (2 * chips)) for i in range(2 * chips)])
+    low, high = jnp.where(lower, fields, far), jnp.where(lower, far, fields)
+    fields = jnp.concatenate([low[:, None], high[:, None]], axis=1).reshape(-1, xlen, ylen)
+
+    force = to_blocks(forcing.reshape(zlen, xlen, ylen))
+    fields = to_blocks(fields)
+    fields = call(
+        functools.partial(arrange_kernel, zpart),
+        jax.ShapeDtypeStruct((3, ROWS, zlen, LANES), f32),
+        (fields,),
+        flags,
+        name="arrange",
+    )
+    near = exchange(fields)
+    region = jax.ShapeDtypeStruct((3, 3 * ROWS, zlen, LANES), f32)
+    coef = call(prep_kernel, region, (fields, *near), flags, name="prep")
+    windows = []
+    for k in range(0, chips, spw):
+        part = force[k : k + spw]
+        windows.append((part, *exchange(part)))
+
+    wide = pltpu.VMEM((3 * ROWS + 1, zlen + 2 * ROWS, LANES), f32)
+    scratch = (wide, wide, pltpu.VMEM((3 * ROWS, zlen, LANES), f32))
+    sweeps = spw * SWEEPS
+    flops = 10 * sweeps * 2 * ROWS * zlen * LANES
+
+    def window(state, beside, part):
+        return call(
+            window_kernel,
+            jax.ShapeDtypeStruct((spw, ROWS, zlen, LANES), f32),
+            (state, *beside, *part, coef),
+            flags,
+            scratch,
+            flops,
+            name="window",
+        )
+
+    start = fields[0]
+    state, beside = start, (near[0][0], near[1][0])
+    for stage in range(2):
+        outs = []
+        for k, part in enumerate(windows):
+            if k or stage:
+                beside = exchange(state)
+            outs.append(window(state, beside, part))
+            state = outs[-1][-1]
+        if stage == 0:
+            state = jnp.where(lower, start, lax.ppermute(state, both, hop))
+
+    result = jnp.concatenate(outs)
+    result = lax.all_to_all(result, "tm", 0, 0, axis_index_groups=groups, tiled=True)
+    half = chips // 2
+    keep = lax.dynamic_slice_in_dim(result, s * half, half)
+    send = lax.dynamic_slice_in_dim(result, (1 - s) * half, half)
+    got = lax.ppermute(send, "space", cores)
+    out = call(
+        functools.partial(unformat_kernel, blocks),
+        jax.ShapeDtypeStruct((zlen, xlen, ylen), f32),
+        (keep.reshape(-1, LANES), got.reshape(-1, LANES)),
+        flags,
+        name="unformat",
+    )
+    return out[None]
+
+
+def per_device(forcing, initial, diffusion, drift):
+    tm, space = lax.axis_size("tm"), lax.axis_size("space")
+    zpart, xlen, ylen = initial.shape
+    chips, spw = tm // 2, 2 * ROWS // SWEEPS
+    along_y = (
+        tm == NT
+        and space == 2
+        and forcing.shape == (1, tm * zpart, xlen, ylen)
+        and 2 * xlen == LANES
+        and ylen == LANES
+        and ylen * space == 2 * ROWS * 2 * chips
+        and chips % spw == 0
+        and chips * zpart % ROWS == 0
+    )
+    plan = split_along_y if along_y else split_along_z
+    return plan(forcing, initial, diffusion, drift)
 
 
 def solution(mesh):

time: 736 us -> 324 us (0.44)
  waiting for transfers between devices: 408 us -> 83.7 us
  Pallas kernels: 0 us -> 153 us
  starting transfers between devices: 188 us -> 59.1 us
  blocking collectives: 58.7 us -> 0 us
  other arithmetic: 42.1 us -> 8.96 us
  local copies, waits for them, and re-layouts: 34.5 us -> 17.9 us
    ppermute x68 -> x17, waiting for transfers between devices: 408 us -> 25 us  [the longest x1 17 us: split_along_y(): lax.ppermute(fields, 'tm', [(i, (i + chips) % (2 * chips)) for i in range...]
    pallas_call x0 -> x9, Pallas kernels: none -> 153 us  [call(): pl.pallas_call(kernel, out_shape=out_shape, in_specs=[pl.BlockSpec(memory...]
    ppermute x68 -> x17, starting transfers between devices: 180 us -> 34.9 us  [the longest x12 25 us: exchange(): return (lax.ppermute(x, 'space', cores), lax.ppermute(x, both, across))]
    all_to_all x1 -> x0, blocking collectives: 58.7 us -> none  [per_device(): return lax.all_to_all(result, 'tm', split_axis=0, concat_axis=1, tiled=True)]
    all_to_all x1 -> x3, waiting for transfers between devices: 0.01 us -> 58.7 us  [the longest x2 32.9 us: to_blocks(): lax.all_to_all(whole, 'tm', 0, 0, axis_index_groups=groups, tiled=True)]
    div x64 -> x0, other arithmetic: 36.2 us -> none  [relax_cells(): (source + diffus * beside + drift_rate * upstream) / (1.0 + 6.0 * diffus...]
    all_to_all x1 -> x3, starting transfers between devices: 8.52 us -> 24.2 us  [the longest x1 16 us: split_along_y(): lax.all_to_all(result, 'tm', 0, 0, axis_index_groups=groups, tiled=True)]
    dynamic_slice x32 -> x1, local copies, waits for them, and re-layouts: 16.7 us -> 1.18 us  [split_along_y(): send = lax.dynamic_slice_in_dim(result, (1 - s) * half, half)]
  transfers between devices with their start and end apart: 69 -> 20, of which waited for: 51 -> 9; matrix products, arithmetic and copies ran while one was open for 0% -> 3% of each run, Pallas kernels for 0% -> 15%
where the time goes in v1:
time: 324 us; the launch traced here: 323 us
  Pallas kernels  153 us (47%)
  waiting for transfers between devices  83.7 us (26%)
  starting transfers between devices  59.1 us (18%)
  local copies, waits for them, and re-layouts  17.9 us (6%)
  other arithmetic  8.96 us (3%)
    pallas_call x9, Pallas kernels, call(): pl.pallas_call(kernel, out_shape=out_shape, in_specs=[pl.BlockSpec(memory...  153 us
    all_to_all x2, waiting for transfers between devices, to_blocks(): lax.all_to_all(whole, 'tm', 0, 0, axis_index_groups=groups, tiled=True)  32.9 us
    all_to_all x1, waiting for transfers between devices, split_along_y(): lax.all_to_all(result, 'tm', 0, 0, axis_index_groups=groups, tiled=True)  25.8 us
    ppermute x12, starting transfers between devices, exchange(): return (lax.ppermute(x, 'space', cores), lax.ppermute(x, both, across))  25 us
    ppermute x1, waiting for transfers between devices, split_along_y(): lax.ppermute(fields, 'tm', [(i, (i + chips) % (2 * chips)) for i in range...  17 us
    all_to_all x1, starting transfers between devices, split_along_y(): lax.all_to_all(result, 'tm', 0, 0, axis_index_groups=groups, tiled=True)  16 us
    all_to_all x2, starting transfers between devices, to_blocks(): lax.all_to_all(whole, 'tm', 0, 0, axis_index_groups=groups, tiled=True)  8.22 us
  transfers between devices with their start and end apart: 20, of which 9 were waited for; matrix products, arithmetic and copies ran while one was open for 3% of the time, Pallas kernels for 15%

profile of v1, /device:TPU:0, one launch (start us, length us, event | category | flops | bytes accessed | tf_op | source)
XLA Modules:
  0.0 322.7 jit_solution(12604624280681241900)
XLA Ops:
  1.1 4.1 %collective-permute-start = (f32[3,4,64,128]{3,2,1,0:T(8,128)S(1)}, f32[3,4,64,128]{3,2,1,0:T(8,128)S(1)}, u32[]{:S(2)}, u32[]{:S(2)}) collective-permute-start(f32[3,4,64,128]{3,2,1,0:T(8,128)S(1)} %pad_maximum_fusion.2), channel_id=1, source_target_pairs={{0,16},{2,18},{4,20},{6,22},{8,24},{10,26},{12,28},{14,30},{16,0},... | collective-permute-start | bytes 1179656 | tf_op jit(solution)/shard_map/ppermute | solution.py:312
  5.7 17.0 %collective-permute-done = f32[3,4,64,128]{3,2,1,0:T(8,128)S(1)} collective-permute-done((f32[3,4,64,128]{3,2,1,0:T(8,128)S(1)}, f32[3,4,64,128]{3,2,1,0:T(8,128)S(1)}, u32[]{:S(2)}, u32[]{:S(2)}) %collective-permute-start) | collective-permute-done | bytes 393248 | tf_op jit(solution)/shard_map/ppermute | solution.py:312
  24.8 4.1 %format.2 = (f32[768,128]{1,0:T(8,128)}, f32[768,128]{1,0:T(8,128)}) custom-call(s32[3]{0:T(128)} %pad_add_fusion.flags, f32[24,64,128]{2,1,0:T(8,128)} %bitcast.31), custom_call_target="tpu_custom_call" | custom-call | flops 1572864 | bytes 1572864 | tf_op jit(solution)/shard_map/format/pallas_call | solution.py:89
  28.9 8.8 %format.3 = (f32[2048,128]{1,0:T(8,128)}, f32[2048,128]{1,0:T(8,128)}) custom-call(s32[3]{0:T(128)} %pad_add_fusion.flags, f32[64,64,128]{2,1,0:T(8,128)} %bitcast.32), custom_call_target="tpu_custom_call" | custom-call | flops 4194304 | bytes 4194304 | tf_op jit(solution)/shard_map/format/pallas_call | solution.py:89
  39.1 3.9 %all-to-all-start = ((f32[8,8,24,128]{3,2,1,0:T(8,128)}), f32[8,8,24,128]{3,2,1,0:T(8,128)S(1)}, u32[]{:S(2)}, u32[]{:S(2)}) async-start(f32[8,8,24,128]{3,2,1,0:T(8,128)} %bitcast.8), calls=%async_computation | async-start | bytes 1572864 | tf_op jit(solution)/shard_map/all_to_all | solution.py:309
  44.5 10.4 %all-to-all-done.got = f32[8,8,24,128]{3,2,1,0:T(8,128)S(1)} async-done(((f32[8,8,24,128]{3,2,1,0:T(8,128)}), f32[8,8,24,128]{3,2,1,0:T(8,128)S(1)}, u32[]{:S(2)}, u32[]{:S(2)}) %all-to-all-start) | async-done | bytes 786464 | tf_op jit(solution)/shard_map/all_to_all | solution.py:309
  55.8 4.3 %all-to-all-start.1 = ((f32[8,8,64,128]{3,2,1,0:T(8,128)}), f32[8,8,64,128]{3,2,1,0:T(8,128)}, u32[]{:S(2)}, u32[]{:S(2)}) async-start(f32[8,8,64,128]{3,2,1,0:T(8,128)} %bitcast.13), calls=%async_computation.1 | async-start | bytes 4194304 | tf_op jit(solution)/shard_map/all_to_all | solution.py:309
  60.2 2.3 arrange.1.own
  64.1 22.5 %all-to-all-done.1 = f32[8,8,64,128]{3,2,1,0:T(8,128)} async-done(((f32[8,8,64,128]{3,2,1,0:T(8,128)}), f32[8,8,64,128]{3,2,1,0:T(8,128)}, u32[]{:S(2)}, u32[]{:S(2)}) %all-to-all-start.1) | async-done | bytes 2097184 | tf_op jit(solution)/shard_map/all_to_all | solution.py:309
  90.7 4.0 %collective-permute-start.9 = (f32[4,8,64,128]{3,2,1,0:T(8,128)S(1)}, f32[4,8,64,128]{3,2,1,0:T(8,128)}, u32[]{:S(2)}, u32[]{:S(2)}) collective-permute-start(f32[4,8,64,128]{3,2,1,0:T(8,128)S(1)} %get-tuple-element.15.f_own), channel_id=1, source_target_pairs={{0,1},{1,0},{2,3},{3,2},{4,5},{5,4},{6,7},{7,6},{8,9},{9,8},{10,11... | collective-permute-start | bytes 3145736 | tf_op jit(solution)/shard_map/ppermute | solution.py:298
  96.5 4.8 %prep.1.coef = f32[3,24,64,128]{3,2,1,0:T(8,128)} custom-call(s32[3]{0:T(128)} %pad_add_fusion.flags, f32[3,8,64,128]{3,2,1,0:T(8,128)} %arrange.1.own, f32[3,8,64,128]{3,2,1,0:T(8,128)} %collective-permute-done.2.core, f32[3,8,64,128]{3,2,1,0:T(8,128)} %collective-permute-done.3.link), custom_call_target="tpu_custom_call" | custom-call | flops 4718592 | bytes 4718592 | tf_op jit(solution)/shard_map/prep/pallas_call | solution.py:89
  104.6 31.1 %window.4 = f32[4,8,64,128]{3,2,1,0:T(8,128)} custom-call(s32[3]{0:T(128)} %pad_add_fusion.flags, f32[8,64,128]{2,1,0:T(8,128)} %slice_bitcast_fusion.5.own, f32[8,64,128]{2,1,0:T(8,128)} %slice_bitcast_fusion.4.core, f32[8,64,128]{2,1,0:T(8,128)} %slice_bitcast_fusion.3.link, f32[4,8,64,128]{3,2,1,0:T(8,128)} %copy-done.1, ...), custom_call_target="tpu_custom_call" | custom-call | flops 20971520 | bytes 7340032 | tf_op jit(solution)/shard_map/window/pallas_call | solution.py:89
  139.7 31.1 %window.5 = f32[4,8,64,128]{3,2,1,0:T(8,128)} custom-call(s32[3]{0:T(128)} %pad_add_fusion.flags, f32[8,64,128]{2,1,0:T(8,128)} %copy-done.7, f32[8,64,128]{2,1,0:T(8,128)} %copy-done.11, f32[8,64,128]{2,1,0:T(8,128)} %copy-done.13, f32[4,8,64,128]{3,2,1,0:T(8,128)} %copy-done, f32[4,8,64,128]{3,2,1,0:T(8,128)} %collective-permute-done.9.f_core, ...), custom_call_target="tpu_custom_call" | custom-call | flops 20971520 | bytes 7340032 | tf_op jit(solution)/shard_map/window/pallas_call | solution.py:89
  171.9 5.3 %collective-permute-start.11 = (f32[8,64,128]{2,1,0:T(8,128)S(1)}, f32[8,64,128]{2,1,0:T(8,128)S(1)}, u32[]{:S(2)}, u32[]{:S(2)}) collective-permute-start(f32[8,64,128]{2,1,0:T(8,128)S(1)} %slice_bitcast_fusion.1), channel_id=1, source_target_pairs={{0,16},{1,17},{2,18},{3,19},{4,20},{5,21},{6,22},{7,23},{8,24},{9,... | collective-permute-start | bytes 786440 | tf_op jit(solution)/shard_map/ppermute | solution.py:359
  177.2 3.9 %collective-permute-done.11 = f32[8,64,128]{2,1,0:T(8,128)S(1)} collective-permute-done((f32[8,64,128]{2,1,0:T(8,128)S(1)}, f32[8,64,128]{2,1,0:T(8,128)S(1)}, u32[]{:S(2)}, u32[]{:S(2)}) %collective-permute-start.11) | collective-permute-done | bytes 262176 | tf_op jit(solution)/shard_map/ppermute | solution.py:359
  182.1 5.6 %collective-permute-start.12 = (f32[8,64,128]{2,1,0:T(8,128)S(1)}, f32[8,64,128]{2,1,0:T(8,128)S(1)}, u32[]{:S(2)}, u32[]{:S(2)}) collective-permute-start(f32[8,64,128]{2,1,0:T(8,128)S(1)} %broadcast_select_fusion.own), channel_id=1, source_target_pairs={{0,1},{1,0},{2,3},{3,2},{4,5},{5,4},{6,7},{7,6},{8,9},{9,8},{10,11... | collective-permute-start | bytes 786440 | tf_op jit(solution)/shard_map/ppermute | solution.py:298
  190.3 31.1 %window.6 = f32[4,8,64,128]{3,2,1,0:T(8,128)} custom-call(s32[3]{0:T(128)} %pad_add_fusion.flags, f32[8,64,128]{2,1,0:T(8,128)} %copy-done.9, f32[8,64,128]{2,1,0:T(8,128)} %copy-done.14, f32[8,64,128]{2,1,0:T(8,128)} %copy-done.16, f32[4,8,64,128]{3,2,1,0:T(8,128)} %copy-done.1, f32[4,8,64,128]{3,2,1,0:T(8,128)} %collective-permute-done.5.f_core, ...), custom_call_target="tpu_custom_call" | custom-call | flops 20971520 | bytes 7340032 | tf_op jit(solution)/shard_map/window/pallas_call | solution.py:89
  222.4 8.8 %collective-permute-start.14 = (f32[8,64,128]{2,1,0:T(8,128)S(1)}, f32[8,64,128]{2,1,0:T(8,128)S(1)}, u32[]{:S(2)}, u32[]{:S(2)}) collective-permute-start(f32[8,64,128]{2,1,0:T(8,128)S(1)} %slice_bitcast_fusion.own), channel_id=1, source_target_pairs={{0,1},{1,0},{2,3},{3,2},{4,5},{5,4},{6,7},{7,6},{8,9},{9,8},{10,11... | collective-permute-start | bytes 786440 | tf_op jit(solution)/shard_map/ppermute | solution.py:298
  233.8 31.1 %window.7 = f32[4,8,64,128]{3,2,1,0:T(8,128)} custom-call(s32[3]{0:T(128)} %pad_add_fusion.flags, f32[8,64,128]{2,1,0:T(8,128)} %copy-done.8, f32[8,64,128]{2,1,0:T(8,128)} %copy-done.12, f32[8,64,128]{2,1,0:T(8,128)} %copy-done.15, f32[4,8,64,128]{3,2,1,0:T(8,128)} %copy-done, f32[4,8,64,128]{3,2,1,0:T(8,128)} %collective-permute-done.9.f_core, ...), custom_call_target="tpu_custom_call" | custom-call | flops 20971520 | bytes 7340032 | tf_op jit(solution)/shard_map/window/pallas_call | solution.py:89
  264.9 2.7 pad_maximum_fusion
  267.6 16.0 %all-to-all-start.2 = ((f32[8,8,64,128]{3,2,1,0:T(8,128)}), f32[8,8,64,128]{3,2,1,0:T(8,128)S(1)}, u32[]{:S(2)}, u32[]{:S(2)}) async-start(f32[8,8,64,128]{3,2,1,0:T(8,128)} %pad_maximum_fusion), calls=%async_computation.2 | async-start | bytes 4194304 | tf_op jit(solution)/shard_map/all_to_all | solution.py:362
  283.6 25.8 %all-to-all-done.2 = f32[8,8,64,128]{3,2,1,0:T(8,128)S(1)} async-done(((f32[8,8,64,128]{3,2,1,0:T(8,128)}), f32[8,8,64,128]{3,2,1,0:T(8,128)S(1)}, u32[]{:S(2)}, u32[]{:S(2)}) %all-to-all-start.2) | async-done | bytes 2097184 | tf_op jit(solution)/shard_map/all_to_all | solution.py:362
  310.6 2.7 collective-permute-done.16
  314.2 8.5 %unformat.1 = f32[64,64,128]{2,1,0:T(8,128)} custom-call(s32[3]{0:T(128)} %pad_add_fusion.flags, f32[2048,128]{1,0:T(8,128)} %bitcast.30, f32[2048,128]{1,0:T(8,128)} %bitcast.33), custom_call_target="tpu_custom_call" | custom-call | flops 4194304 | bytes 4194304 | tf_op jit(solution)/shard_map/unformat/pallas_call | solution.py:89
  (76 shorter events, 32.7 us)
Async XLA Ops:
  1.1 21.7 %collective-permute-start = (f32[3,4,64,128]{3,2,1,0:T(8,128)S(1)}, f32[3,4,64,128]{3,2,1,0:T(8,128)S(1)}, u32[]{:S(2)}, u32[]{:S(2)}) collective-permute-start(f32[3,4,64,128]{3,2,1,0:T(8,128)S(1)} %pad_maximum_fusion.2), channel_id=1, source_target_pairs={{0,16},{2,18},{4,20},{6,22},{8,24},{10,26},{12,28},{14,30},{16,0},... | collective-permute-start | bytes 1179656 | tf_op jit(solution)/shard_map/ppermute | solution.py:312
  28.9 9.2 %collective-permute-start.1 = (f32[768,128]{1,0:T(8,128)}, f32[768,128]{1,0:T(8,128)S(1)}, u32[]{:S(2)}, u32[]{:S(2)}) collective-permute-start(f32[768,128]{1,0:T(8,128)} %get-tuple-element.10), channel_id=1, source_target_pairs={{0,1},{1,0},{2,3},{3,2},{4,5},{5,4},{6,7},{7,6},{8,9},{9,8},{10,11... | collective-permute-start | bytes 1179656 | tf_op jit(solution)/shard_map/ppermute | solution.py:306
  37.7 5.3 %collective-permute-start.4 = (f32[2048,128]{1,0:T(8,128)}, f32[2048,128]{1,0:T(8,128)S(1)}, u32[]{:S(2)}, u32[]{:S(2)}) collective-permute-start(f32[2048,128]{1,0:T(8,128)} %get-tuple-element.12), channel_id=1, source_target_pairs={{0,1},{1,0},{2,3},{3,2},{4,5},{5,4},{6,7},{7,6},{8,9},{9,8},{10,11... | collective-permute-start | bytes 3145736 | tf_op jit(solution)/shard_map/ppermute | solution.py:306
  39.1 15.8 %all-to-all-start = ((f32[8,8,24,128]{3,2,1,0:T(8,128)}), f32[8,8,24,128]{3,2,1,0:T(8,128)S(1)}, u32[]{:S(2)}, u32[]{:S(2)}) async-start(f32[8,8,24,128]{3,2,1,0:T(8,128)} %bitcast.8), calls=%async_computation | async-start | bytes 1572864 | tf_op jit(solution)/shard_map/all_to_all | solution.py:309
  55.8 30.7 %all-to-all-start.1 = ((f32[8,8,64,128]{3,2,1,0:T(8,128)}), f32[8,8,64,128]{3,2,1,0:T(8,128)}, u32[]{:S(2)}, u32[]{:S(2)}) async-start(f32[8,8,64,128]{3,2,1,0:T(8,128)} %bitcast.13), calls=%async_computation.1 | async-start | bytes 4194304 | tf_op jit(solution)/shard_map/all_to_all | solution.py:309
  62.4 28.3 %collective-permute-start.2 = (f32[3,8,64,128]{3,2,1,0:T(8,128)}, f32[3,8,64,128]{3,2,1,0:T(8,128)}, u32[]{:S(2)}, u32[]{:S(2)}) collective-permute-start(f32[3,8,64,128]{3,2,1,0:T(8,128)} %arrange.1.own), channel_id=1, source_target_pairs={{0,1},{1,0},{2,3},{3,2},{4,5},{5,4},{6,7},{7,6},{8,9},{9,8},{10,11... | collective-permute-start | bytes 2359304 | tf_op jit(solution)/shard_map/ppermute | solution.py:298
  62.4 34.0 %collective-permute-start.3 = (f32[3,8,64,128]{3,2,1,0:T(8,128)}, f32[3,8,64,128]{3,2,1,0:T(8,128)}, u32[]{:S(2)}, u32[]{:S(2)}) collective-permute-start(f32[3,8,64,128]{3,2,1,0:T(8,128)} %arrange.1.own), channel_id=1, source_target_pairs={{1,3},{3,1},{17,19},{19,17},{2,6},{6,2},{18,22},{22,18},{7,5},{5,7... | collective-permute-start | bytes 2359304 | tf_op jit(solution)/shard_map/ppermute | solution.py:298
  88.2 13.0 %copy-start = (f32[4,8,64,128]{3,2,1,0:T(8,128)}, f32[4,8,64,128]{3,2,1,0:T(8,128)S(1)}, u32[]{:S(2)}) copy-start(f32[4,8,64,128]{3,2,1,0:T(8,128)S(1)} %get-tuple-element.15.f_own) | copy-start | bytes 3145732
  88.3 13.0 %copy-start.1 = (f32[4,8,64,128]{3,2,1,0:T(8,128)}, f32[4,8,64,128]{3,2,1,0:T(8,128)S(1)}, u32[]{:S(2)}) copy-start(f32[4,8,64,128]{3,2,1,0:T(8,128)S(1)} %get-tuple-element.16.f_own) | copy-start | bytes 3145732
  88.3 16.3 %collective-permute-start.5 = (f32[4,8,64,128]{3,2,1,0:T(8,128)S(1)}, f32[4,8,64,128]{3,2,1,0:T(8,128)}, u32[]{:S(2)}, u32[]{:S(2)}) collective-permute-start(f32[4,8,64,128]{3,2,1,0:T(8,128)S(1)} %get-tuple-element.16.f_own), channel_id=1, source_target_pairs={{0,1},{1,0},{2,3},{3,2},{4,5},{5,4},{6,7},{7,6},{8,9},{9,8},{10,11... | collective-permute-start | bytes 3145736 | tf_op jit(solution)/shard_map/ppermute | solution.py:298
  88.3 16.2 %collective-permute-start.6 = (f32[4,8,64,128]{3,2,1,0:T(8,128)S(1)}, f32[4,8,64,128]{3,2,1,0:T(8,128)}, u32[]{:S(2)}, u32[]{:S(2)}) collective-permute-start(f32[4,8,64,128]{3,2,1,0:T(8,128)S(1)} %get-tuple-element.16.f_own), channel_id=1, source_target_pairs={{1,3},{3,1},{17,19},{19,17},{2,6},{6,2},{18,22},{22,18},{7,5},{5,7... | collective-permute-start | bytes 3145736 | tf_op jit(solution)/shard_map/ppermute | solution.py:298
  90.0 47.8 %collective-permute-start.10 = (f32[4,8,64,128]{3,2,1,0:T(8,128)S(1)}, f32[4,8,64,128]{3,2,1,0:T(8,128)S(1)}, u32[]{:S(2)}, u32[]{:S(2)}) collective-permute-start(f32[4,8,64,128]{3,2,1,0:T(8,128)S(1)} %get-tuple-element.15.f_own), channel_id=1, source_target_pairs={{1,3},{3,1},{17,19},{19,17},{2,6},{6,2},{18,22},{22,18},{7,5},{5,7... | collective-permute-start | bytes 3145736 | tf_op jit(solution)/shard_map/ppermute | solution.py:298
  90.7 47.1 %collective-permute-start.9 = (f32[4,8,64,128]{3,2,1,0:T(8,128)S(1)}, f32[4,8,64,128]{3,2,1,0:T(8,128)}, u32[]{:S(2)}, u32[]{:S(2)}) collective-permute-start(f32[4,8,64,128]{3,2,1,0:T(8,128)S(1)} %get-tuple-element.15.f_own), channel_id=1, source_target_pairs={{0,1},{1,0},{2,3},{3,2},{4,5},{5,4},{6,7},{7,6},{8,9},{9,8},{10,11... | collective-permute-start | bytes 3145736 | tf_op jit(solution)/shard_map/ppermute | solution.py:298
  136.6 1.7 collective-permute-start.7
  137.1 1.2 collective-permute-start.8
  171.9 9.2 %collective-permute-start.11 = (f32[8,64,128]{2,1,0:T(8,128)S(1)}, f32[8,64,128]{2,1,0:T(8,128)S(1)}, u32[]{:S(2)}, u32[]{:S(2)}) collective-permute-start(f32[8,64,128]{2,1,0:T(8,128)S(1)} %slice_bitcast_fusion.1), channel_id=1, source_target_pairs={{0,16},{1,17},{2,18},{3,19},{4,20},{5,21},{6,22},{7,23},{8,24},{9,... | collective-permute-start | bytes 786440 | tf_op jit(solution)/shard_map/ppermute | solution.py:359
  182.1 6.8 %collective-permute-start.12 = (f32[8,64,128]{2,1,0:T(8,128)S(1)}, f32[8,64,128]{2,1,0:T(8,128)S(1)}, u32[]{:S(2)}, u32[]{:S(2)}) collective-permute-start(f32[8,64,128]{2,1,0:T(8,128)S(1)} %broadcast_select_fusion.own), channel_id=1, source_target_pairs={{0,1},{1,0},{2,3},{3,2},{4,5},{5,4},{6,7},{7,6},{8,9},{9,8},{10,11... | collective-permute-start | bytes 786440 | tf_op jit(solution)/shard_map/ppermute | solution.py:298
  187.7 1.2 collective-permute-start.13
  222.4 10.0 %copy-start.8 = (f32[8,64,128]{2,1,0:T(8,128)}, f32[8,64,128]{2,1,0:T(8,128)S(1)}, u32[]{:S(2)}) copy-start(f32[8,64,128]{2,1,0:T(8,128)S(1)} %slice_bitcast_fusion.own) | copy-start | bytes 786436
  222.4 42.5 %copy-start.2 = (f32[4,8,64,128]{3,2,1,0:T(8,128)S(1)}, f32[4,8,64,128]{3,2,1,0:T(8,128)}, u32[]{:S(2)}) copy-start(f32[4,8,64,128]{3,2,1,0:T(8,128)} %window.6) | copy-start | bytes 3145732
  222.4 10.0 %collective-permute-start.14 = (f32[8,64,128]{2,1,0:T(8,128)S(1)}, f32[8,64,128]{2,1,0:T(8,128)S(1)}, u32[]{:S(2)}, u32[]{:S(2)}) collective-permute-start(f32[8,64,128]{2,1,0:T(8,128)S(1)} %slice_bitcast_fusion.own), channel_id=1, source_target_pairs={{0,1},{1,0},{2,3},{3,2},{4,5},{5,4},{6,7},{7,6},{8,9},{9,8},{10,11... | collective-permute-start | bytes 786440 | tf_op jit(solution)/shard_map/ppermute | solution.py:298
  231.2 1.2 collective-permute-start.15
  267.6 41.7 %all-to-all-start.2 = ((f32[8,8,64,128]{3,2,1,0:T(8,128)}), f32[8,8,64,128]{3,2,1,0:T(8,128)S(1)}, u32[]{:S(2)}, u32[]{:S(2)}) async-start(f32[8,8,64,128]{3,2,1,0:T(8,128)} %pad_maximum_fusion), calls=%async_computation.2 | async-start | bytes 4194304 | tf_op jit(solution)/shard_map/all_to_all | solution.py:362
  310.6 2.7 collective-permute-start.16
  (13 other events, 30.1 us)

commit v2 on v1

v2 whole, which is shorter than its diff:
```python
import functools
import math

import jax
import jax.numpy as jnp
from jax import lax
from jax.experimental import pallas as pl
from jax.experimental.pallas import tpu as pltpu
from jax.sharding import PartitionSpec as P


NT = 16
SWEEPS = 4
LANES = 128
ROWS = 8
FILL = 4
BATCH = 24


def padded(shard, sides, width):
    for axis, dim in sides:
        size, length = (lax.axis_size(axis), shard.shape[dim])
        up = [(i, (i + 1) % size) for i in range(size - 1)]
        down = [(j, i) for i, j in up]
        last = lax.slice_in_dim(shard, length - width, length, axis=dim)
        leading = lax.slice_in_dim(shard, 0, width, axis=dim)
        before = lax.ppermute(last, axis, up)
        after = lax.ppermute(leading, axis, down)
        shard = jnp.concatenate([before, shard, after], axis=dim)
    return shard


def relax_cells(field, source, diffus, drift_rate):
    widened = jnp.pad(field, ((0, 0), (1, 1), (0, 0)))
    beside = field[2:, :, 1:-1] + field[:-2, :, 1:-1]
    beside = beside + field[1:-1, :, 2:] + field[1:-1, :, :-2]
    beside = beside + widened[1:-1, 2:, 1:-1] + widened[1:-1, :-2, 1:-1]
    upstream = field[:-2, :, 1:-1]
    return (source + diffus * beside + drift_rate * upstream) / (1.0 + 6.0 * diffus + drift_rate)


def trim_rim(values, margin_cut):
    zlen = values.shape[-3]
    ylen = values.shape[-1]
    return values[..., margin_cut : zlen - margin_cut, :, margin_cut : ylen - margin_cut]


def sweep_block(widened, coef_wide, depth):
    grown = widened[0]
    for inner in range(depth):
        margin_cut = inner + 1
        grown = relax_cells(
            grown,
            trim_rim(widened[1], margin_cut),
            trim_rim(coef_wide[0], margin_cut),
            trim_rim(coef_wide[1], margin_cut),
        )
    return grown


def split_along_z(forcing, initial, diffusion, drift):
    xparts = lax.axis_size("tm") // NT
    slabs = lax.all_to_all(forcing, "tm", split_axis=1, concat_axis=0, tiled=True)
    zcells = slabs.shape[1]
    xpart = slabs.shape[2]
    ycells = slabs.shape[3]
    slabs = slabs.reshape(NT, xparts, zcells, xpart, ycells).transpose(0, 2, 1, 3, 4)
    slabs = slabs.reshape(NT, zcells, xparts * xpart, ycells)
    coeffs = jnp.stack((diffusion, drift))
    coef_wide = padded(coeffs, (("tm", 1), ("space", 3)), SWEEPS)

    def advance(current, forcing_now):
        source = current + forcing_now
        field = current
        widened = padded(jnp.stack((field, source)), (("tm", 1), ("space", 3)), SWEEPS)
        field = sweep_block(widened, coef_wide, SWEEPS)
        return (field, field)

    _, result = lax.scan(advance, initial, slabs)
    result = result.reshape(NT, zcells, xparts, xpart, ycells).transpose(0, 2, 1, 3, 4)
    result = result.reshape(NT * xparts, zcells, xpart, ycells)
    return lax.all_to_all(result, "tm", split_axis=0, concat_axis=1, tiled=True)


def gray(i):
    return i ^ (i >> 1)


def call(kernel, out_shape, operands, flags, scratch=(), flops=0, part=None):
    specs = [pl.BlockSpec(memory_space=pltpu.VMEM)] * len(operands)
    grid = ()
    if part:
        which, at, shape = part
        grid = (1,)
        specs[which] = pl.BlockSpec(shape, lambda _: (at,) + (0,) * (len(shape) - 1))
    size = sum(x.size * x.dtype.itemsize for x in operands)
    shapes = out_shape if isinstance(out_shape, (tuple, list)) else (out_shape,)
    size += sum(functools.reduce(lambda a, b: a * b, x.shape) * 4 for x in shapes)
    return pl.pallas_call(
        kernel,
        grid=grid,
        out_shape=out_shape,
        in_specs=[pl.BlockSpec(memory_space=pltpu.SMEM)] + specs,
        out_specs=jax.tree.map(lambda _: pl.BlockSpec(memory_space=pltpu.VMEM), out_shape),
        scratch_shapes=list(scratch),
        cost_estimate=pl.CostEstimate(flops=flops or size, bytes_accessed=size, transcendentals=0),
    )(flags, *operands)


def left_lanes():
    return lax.broadcasted_iota(jnp.int32, (ROWS, LANES), 1) < LANES // 2


def swap_lanes(v):
    return pltpu.roll(v, LANES // 2, 1)


def unrolled(count, one):
    depth = math.gcd(count, 4)

    def step(k, carry):
        for j in range(depth):
            one(depth * k + j)
        return carry

    lax.fori_loop(0, count // depth, step, 0)


def format_kernel(blocks, flags, raw, whole, send):
    zrows = raw.shape[0]
    left = left_lanes()

    def body(core):
        def one(pair):
            both = raw[pl.ds(2 * pair, 2)].reshape(LANES, LANES).T
            for r in range(blocks):
                low = both[2 * ROWS * r : 2 * ROWS * r + ROWS]
                high = both[2 * ROWS * r + ROWS : 2 * ROWS * (r + 1)]
                first = jnp.where(left, low, swap_lanes(high))
                second = jnp.where(left, swap_lanes(low), high)
                slot = gray(core * (blocks // 2) + r // 2)
                mine = gray(r) & 1 == core
                to = whole if mine else send
                start = (slot if mine else slot % (blocks // 2)) * ROWS * zrows + 2 * pair
                to[pl.ds(start, ROWS, stride=zrows), :] = first
                to[pl.ds(start + 1, ROWS, stride=zrows), :] = second

        unrolled(zrows // 2, one)

    for core in range(2):
        pl.when(flags[1] == core)(functools.partial(body, core))


def unformat_kernel(blocks, flags, whole, got, out):
    zrows = out.shape[0]
    left = left_lanes()

    def body(core):
        def one(pair):
            columns = []
            for r in range(blocks):
                slot = gray(core * (blocks // 2) + r // 2)
                mine = gray(r) & 1 == core
                src = whole if mine else got
                start = (slot if mine else slot % (blocks // 2)) * ROWS * zrows + 2 * pair
                first = src[pl.ds(start, ROWS, stride=zrows), :]
                second = src[pl.ds(start + 1, ROWS, stride=zrows), :]
                columns.append(jnp.where(left, first, swap_lanes(second)))
                columns.append(jnp.where(left, swap_lanes(first), second))
            both = jnp.concatenate(columns, axis=0).T
            out[pl.ds(2 * pair, 2)] = both.reshape(2, LANES // 2, LANES)

        unrolled(zrows // 2, one)

    for core in range(2):
        pl.when(flags[1] == core)(functools.partial(body, core))


def arrange_kernel(zpart, flags, got, out):
    chips, arrays = got.shape[0], out.shape[0]
    for k in range(arrays):
        for chip in range(chips):
            for upper in range(2):
                rows = pl.ds((2 * k + upper) * zpart, zpart)
                z = (upper * chips + chip) * zpart
                out[k, :, pl.ds(z, zpart), :] = got[chip, :, rows, :]


class Region:
    def __init__(self, even):
        self.even = even
        left = left_lanes()[None]
        self.left = left
        self.other = jnp.logical_xor(left, jnp.full((1, ROWS, LANES), even, jnp.int32) == 1)

    def tiles(self, plane):
        return plane.reshape(-1, ROWS, LANES)

    def plane(self, kind, m, own, core, link):
        back = ROWS - 1 - m
        if kind == "own":
            v = jnp.where(self.left, self.tiles(own[m]), self.tiles(own[back]))
        elif kind == "far":
            c = self.tiles(core[jnp.where(self.even == 1, back, m)])
            n = self.tiles(link[jnp.where(self.even == 1, m, back)])
            v = jnp.where(self.other, c, n)
        else:
            c = self.tiles(core[jnp.where(self.even == 1, m, back)])
            n = self.tiles(link[jnp.where(self.even == 1, back, m)])
            v = pltpu.roll(jnp.where(self.other, n, c), LANES // 2, 2)
        return v.reshape(-1, LANES)

    def fill(self, skip, own, core, link, put):
        def run(kind, start, stop, place):
            def step(k, carry):
                for j in range(FILL):
                    m = FILL * k + j
                    put(place(m), self.plane(kind, m, own, core, link))
                return carry

            lax.fori_loop(start, stop, step, 0)

        groups = ROWS // FILL
        run("own", 0, groups, lambda m: 2 * ROWS + m)
        run("near", 0, jnp.minimum(groups, 2 * groups - skip), lambda m: 2 * ROWS - 1 - m)
        run("far", jnp.minimum(skip, groups), groups, lambda m: m)


def prep_kernel(flags, own, core, link, coef):
    region = Region(flags[0])

    def put_diffusion(i, d):
        coef[0, i] = d

    def put_drift(i, r):
        d = coef[0, i]
        inv = 1.0 / (1.0 + 6.0 * d + r)
        coef[0, i] = d * inv
        coef[1, i] = (d + r) * inv
        coef[2, i] = inv

    region.fill(0, own.at[1], core.at[1], link.at[1], put_diffusion)
    region.fill(0, own.at[2], core.at[2], link.at[2], put_drift)


def window_kernel(done, flags, own, core, link, f_own, f_core, f_link, coef, *rest):
    if done:
        earlier, out, last, va, vb, c = rest
        out[0:done] = earlier[...]
    else:
        out, last, va, vb, c = rest
    steps, planes, zrows = f_core.shape[0], 3 * ROWS, own.shape[2]
    region = Region(flags[0])
    lane = lax.broadcasted_iota(jnp.int32, (ROWS, LANES), 1) % (LANES // 2)
    first_x, last_x = lane == 0, lane == LANES // 2 - 1
    inside = pl.ds(ROWS, zrows)
    ghost = planes + 1
    edge = jnp.zeros((planes + 2, ROWS, LANES), jnp.float32)
    for v in (va, vb):
        v[:, 0:ROWS] = edge
        v[:, zrows + ROWS :] = edge
        v[0, inside] = jnp.zeros((zrows, LANES), jnp.float32)

    def put_field(i, plane):
        va[1 + i, inside] = plane

    region.fill(0, own.at[0], core.at[0], link.at[0], put_field)
    va[ghost, inside] = swap_lanes(va[planes, inside])

    def relax(src, dst, first):
        cells = [(z, i) for z in range(0, zrows, ROWS) for i in reversed(range(first, planes))]
        for lead in range(0, len(cells), BATCH):
            part = cells[lead : lead + BATCH]
            field = [src[1 + i, ROWS + z : 2 * ROWS + z] for z, i in part]
            below = [pltpu.roll(v, 1, 1) for v in field]
            above = [pltpu.roll(v, LANES - 1, 1) for v in field]
            for (z, i), low, high in zip(part, below, above):
                at, rows = ROWS + z, slice(z, z + ROWS)
                zm = src[1 + i, at - 1 : at + ROWS - 1]
                total = src[1 + i, at + 1 : at + ROWS + 1]
                total += src[i, at : at + ROWS] + src[2 + i, at : at + ROWS]
                total += jnp.where(first_x, 0.0, low) + jnp.where(last_x, 0.0, high)
                new = c[i, rows] + coef[0, i, rows] * total + coef[1, i, rows] * zm
                dst[1 + i, at : at + ROWS] = new
        dst[ghost, inside] = swap_lanes(dst[planes, inside])

    def advance(first, step, carry):
        def put_source(i, plane):
            c[i] = coef[2, i] * (va[1 + i, inside] + plane)

        region.fill(SWEEPS * step // FILL, f_own.at[step], f_core.at[step], f_link.at[step], put_source)

        def pair(n, carry):
            relax(va, vb, first)
            relax(vb, va, first)
            return carry

        lax.fori_loop(0, SWEEPS // 2, pair, 0)
        for m in range(ROWS):
            low = region.tiles(va[1 + 2 * ROWS + m, inside])
            high = region.tiles(va[planes - m, inside])
            out[done + step, m] = jnp.where(region.left, low, high).reshape(-1, LANES)
        return carry

    half = steps // 2
    lax.fori_loop(0, half, functools.partial(advance, 1), 0)
    lax.fori_loop(half, steps, functools.partial(advance, SWEEPS * half + 1), 0)
    last[0] = out[done + steps - 1]


def split_along_y(forcing, initial, diffusion, drift):
    f32 = jnp.float32
    chips = lax.axis_size("tm") // 2
    zpart, xlen, ylen = initial.shape
    zlen = forcing.shape[1]
    blocks = ylen // (2 * ROWS)
    spw = 2 * ROWS // SWEEPS
    t, s = lax.axis_index("tm"), lax.axis_index("space")
    device = 2 * (t % chips) + s
    odd = device
    for shift in (1, 2, 4, 8):
        odd = odd ^ (odd >> shift)
    lower = t < chips
    flags = jnp.stack([1 - (odd & 1), s, jnp.int32(0)]).astype(jnp.int32)
    groups = [list(range(chips)), list(range(chips, 2 * chips))]
    both = ("tm", "space")
    across = []
    for b in range(1, 2 * chips - 1, 2):
        for base in (0, 2 * chips):
            i, j = base + gray(b), base + gray(b + 1)
            across += [(i, j), (j, i)]
    hop = [(i, 2 * chips + i) for i in range(2 * chips)]
    cores = [(0, 1), (1, 0)]

    def exchange(x):
        return lax.ppermute(x, "space", cores), lax.ppermute(x, both, across)

    def packed(raw):
        zr = raw.shape[0]
        shapes = [jax.ShapeDtypeStruct((n * ROWS * zr, LANES), f32) for n in (blocks, blocks // 2)]
        whole, send = call(functools.partial(format_kernel, blocks), shapes, (raw,), flags)
        got = lax.ppermute(send, "space", cores)
        whole = lax.dynamic_update_slice_in_dim(whole, got, (1 - s) * got.shape[0], 0)
        return whole.reshape(chips, ROWS, zr, LANES)

    def to_chips(x):
        return lax.all_to_all(x, "tm", 0, 0, axis_index_groups=groups, tiled=True)

    fields = jnp.stack((initial, diffusion, drift))
    far = lax.ppermute(fields, "tm", [(i, (i + chips) % (2 * chips)) for i in range(2 * chips)])
    force = packed(forcing.reshape(zlen, xlen, ylen))
    low, high = jnp.where(lower, fields, far), jnp.where(lower, far, fields)
    fields = jnp.concatenate([low[:, None], high[:, None]], axis=1).reshape(-1, xlen, ylen)
    force = to_chips(force)
    fields, force = lax.optimization_barrier((packed(fields), force))
    fields = to_chips(fields)
    fields = call(
        functools.partial(arrange_kernel, zpart),
        jax.ShapeDtypeStruct((3, ROWS, zlen, LANES), f32),
        (fields,),
        flags,
    )
    near = exchange(fields)
    region = jax.ShapeDtypeStruct((3, 3 * ROWS, zlen, LANES), f32)
    coef = call(prep_kernel, region, (fields, *near), flags)
    halos = [exchange(force[k : k + spw]) for k in range(0, chips, spw)]

    wide = pltpu.VMEM((3 * ROWS + 2, zlen + 2 * ROWS, LANES), f32)
    scratch = (
        wide,
        wide,
        pltpu.VMEM((3 * ROWS, zlen, LANES), f32),
    )
    flops = 10 * spw * SWEEPS * 2 * ROWS * zlen * LANES
    block = jax.ShapeDtypeStruct((1, ROWS, zlen, LANES), f32)

    def window(state, beside, k, earlier):
        done = k * spw
        return call(
            functools.partial(window_kernel, done),
            (jax.ShapeDtypeStruct((done + spw, ROWS, zlen, LANES), f32), block),
            (state, *beside, force, *halos[k], coef, *earlier),
            flags,
            scratch,
            flops,
            part=(3, k, (spw, ROWS, zlen, LANES)),
        )

    state, beside = fields, near
    for stage in range(2):
        earlier = ()
        for k in range(len(halos)):
            if k or stage:
                beside = exchange(state)
            result, state = window(state, beside, k, earlier)
            earlier = (result,)
        if stage == 0:
            state = jnp.where(lower, fields[0:1], lax.ppermute(state, both, hop))

    result = to_chips(result)
    send = lax.dynamic_slice_in_dim(result, (1 - s) * (chips // 2), chips // 2)
    got = lax.ppermute(send, "space", cores)
    out = call(
        functools.partial(unformat_kernel, blocks),
        jax.ShapeDtypeStruct((zlen, xlen, ylen), f32),
        (result.reshape(-1, LANES), got.reshape(-1, LANES)),
        flags,
    )
    return out[None]


def per_device(forcing, initial, diffusion, drift):
    tm, space = lax.axis_size("tm"), lax.axis_size("space")
    zpart, xlen, ylen = initial.shape
    chips, spw = tm // 2, 2 * ROWS // SWEEPS
    along_y = (
        tm == NT
        and space == 2
        and forcing.shape == (1, tm * zpart, xlen, ylen)
        and 2 * xlen == LANES
        and ylen == LANES
        and ylen * space == 2 * ROWS * 2 * chips
        and chips % spw == 0
        and chips * zpart % ROWS == 0
    )
    plan = split_along_y if along_y else split_along_z
    return plan(forcing, initial, diffusion, drift)


def solution(mesh):
    in_specs = (
        P("tm", None, None, "space"),
        P("tm", None, "space"),
        P("tm", None, "space"),
        P("tm", None, "space"),
    )
    out_specs = P("tm", None, None, "space")
    return jax.shard_map(
        per_device, mesh=mesh, in_specs=in_specs, out_specs=out_specs, check_vma=False
    )
```

time: 324 us -> 232 us (0.72)
  Pallas kernels: 153 us -> 69.6 us
  blocking collectives: 0 us -> 23.6 us
  waiting for transfers between devices: 83.7 us -> 68.4 us
  local copies, waits for them, and re-layouts: 17.9 us -> 6.44 us
  other arithmetic: 8.96 us -> 1.81 us
    pallas_call x9, Pallas kernels: 153 us -> 69.6 us  [call(): pl.pallas_call(kernel, grid=grid, out_shape=out_shape, in_specs=[pl.Block...]
    all_to_all x3 -> x2, waiting for transfers between devices: 58.7 us -> 24.4 us  [to_chips(): return lax.all_to_all(x, 'tm', 0, 0, axis_index_groups=groups, tiled=True)]
    all_to_all x0 -> x1, blocking collectives: none -> 23.6 us  [to_chips(): return lax.all_to_all(x, 'tm', 0, 0, axis_index_groups=groups, tiled=True)]
    ppermute x1, waiting for transfers between devices: 17 us -> 28.8 us  [split_along_y(): lax.ppermute(fields, 'tm', [(i, (i + chips) % (2 * chips)) for i in range...]
    ppermute x12, starting transfers between devices: 25 us -> 34.1 us  [exchange(): return (lax.ppermute(x, 'space', cores), lax.ppermute(x, both, across))]
    squeeze x6 -> x0, local copies, waits for them, and re-layouts: 7.98 us -> none  [the longest x2 3.37 us: split_along_y(): state, beside = (start, (near[0][0], near[1][0]))]
    ppermute x3, waiting for transfers between devices: 3.91 us -> 8.64 us  [the longest x2 4.43 us: packed(): got = lax.ppermute(send, 'space', cores)]
    ppermute x3, starting transfers between devices: 5.76 us -> 1.94 us  [the longest x1 1.45 us: split_along_y(): state = jnp.where(lower, fields[0:1], lax.ppermute(state, both, hop))]
  transfers between devices with their start and end apart: 20 -> 19, of which waited for: 9 -> 9; matrix products, arithmetic and copies ran while one was open for 3% -> 1% of each run, Pallas kernels for 15% -> 8%
where the time goes in v2:
time: 232 us
  Pallas kernels  69.6 us (30%)
  waiting for transfers between devices  68.4 us (29%)
  starting transfers between devices  61.7 us (27%)
  blocking collectives  23.6 us (10%)
  local copies, waits for them, and re-layouts  6.44 us (3%)
    pallas_call x9, Pallas kernels, call(): pl.pallas_call(kernel, grid=grid, out_shape=out_shape, in_specs=[pl.Block...  69.6 us
    ppermute x12, starting transfers between devices, exchange(): return (lax.ppermute(x, 'space', cores), lax.ppermute(x, both, across))  34.1 us
    ppermute x1, waiting for transfers between devices, split_along_y(): lax.ppermute(fields, 'tm', [(i, (i + chips) % (2 * chips)) for i in range...  28.8 us
    all_to_all x2, waiting for transfers between devices, to_chips(): return lax.all_to_all(x, 'tm', 0, 0, axis_index_groups=groups, tiled=True)  24.4 us
    all_to_all x1, blocking collectives, to_chips(): return lax.all_to_all(x, 'tm', 0, 0, axis_index_groups=groups, tiled=True)  23.6 us
    all_to_all x2, starting transfers between devices, to_chips(): return lax.all_to_all(x, 'tm', 0, 0, axis_index_groups=groups, tiled=True)  23 us
  transfers between devices with their start and end apart: 19, of which 9 were waited for; matrix products, arithmetic and copies ran while one was open for 1% of the time, Pallas kernels for 8%

profile of v2, /device:TPU:0, one launch (start us, length us, event | category | flops | bytes accessed | tf_op | source)
XLA Modules:
  0.0 231.7 jit_solution(5776959458053645514)
XLA Ops:
  0.7 5.9 %shard_map.47 = (f32[4096,128]{1,0:T(8,128)}, f32[2048,128]{1,0:T(8,128)}) custom-call(s32[3]{0:T(128)} %pad_add_fusion.flags, f32[64,64,128]{2,1,0:T(8,128)} %bitcast.18), custom_call_target="tpu_custom_call" | custom-call | flops 5242880 | bytes 5242880 | tf_op jit(solution)/shard_map/pallas_call | solution.py:99
  7.0 2.5 %collective-permute-done.2 = f32[2048,128]{1,0:T(8,128)S(1)} collective-permute-done((f32[2048,128]{1,0:T(8,128)}, f32[2048,128]{1,0:T(8,128)S(1)}, u32[]{:S(2)}, u32[]{:S(2)}) %collective-permute-start.2) | collective-permute-done | bytes 1048608 | tf_op jit(solution)/shard_map/ppermute | solution.py:342
  10.6 6.2 %all-to-all-start = ((f32[8,8,64,128]{3,2,1,0:T(8,128)}), f32[8,8,64,128]{3,2,1,0:T(8,128)S(1)}, u32[]{:S(2)}, u32[]{:S(2)}) async-start(f32[8,8,64,128]{3,2,1,0:T(8,128)} %bitcast.19), calls=%async_computation | async-start | bytes 4194304 | tf_op jit(solution)/shard_map/all_to_all | solution.py:347
  16.9 2.7 %collective-permute-start = (f32[3,4,64,128]{3,2,1,0:T(8,128)S(1)}, f32[3,4,64,128]{3,2,1,0:T(8,128)S(1)}, u32[]{:S(2)}, u32[]{:S(2)}) collective-permute-start(f32[3,4,64,128]{3,2,1,0:T(8,128)S(1)} %pad_maximum_fusion.1), channel_id=1, source_target_pairs={{0,16},{2,18},{4,20},{6,22},{8,24},{10,26},{12,28},{14,30},{16,0},... | collective-permute-start | bytes 1179656 | tf_op jit(solution)/shard_map/ppermute | solution.py:350
  19.5 28.8 %collective-permute-done = f32[3,4,64,128]{3,2,1,0:T(8,128)S(1)} collective-permute-done((f32[3,4,64,128]{3,2,1,0:T(8,128)S(1)}, f32[3,4,64,128]{3,2,1,0:T(8,128)S(1)}, u32[]{:S(2)}, u32[]{:S(2)}) %collective-permute-start) | collective-permute-done | bytes 393248 | tf_op jit(solution)/shard_map/ppermute | solution.py:350
  49.4 3.0 %shard_map.46 = (f32[1536,128]{1,0:T(8,128)}, f32[768,128]{1,0:T(8,128)}) custom-call(s32[3]{0:T(128)} %pad_add_fusion.flags, f32[24,64,128]{2,1,0:T(8,128)} %bitcast.17), custom_call_target="tpu_custom_call" | custom-call | flops 1966080 | bytes 1966080 | tf_op jit(solution)/shard_map/pallas_call | solution.py:99
  52.4 1.9 collective-permute-done.1
  55.1 23.6 %all_to_all.15.got = f32[8,8,24,128]{3,2,1,0:T(8,128)} all-to-all(f32[8,8,24,128]{3,2,1,0:T(8,128)} %bitcast.21), channel_id=1, replica_groups={{0,2,4,6,8,10,12,14},{16,18,20,22,24,26,28,30},{1,3,5,7,9,11,13,15},{17..., dimensions={0} | all-to-all | bytes 1572864 | tf_op jit(solution)/shard_map/all_to_all | solution.py:347
  78.7 2.2 shard_map.48.own
  80.9 1.7 collective-permute-start.4
  86.8 5.7 %collective-permute-start.9 = (f32[4,8,64,128]{3,2,1,0:T(8,128)S(1)}, f32[4,8,64,128]{3,2,1,0:T(8,128)S(1)}, u32[]{:S(2)}, u32[]{:S(2)}) collective-permute-start(f32[4,8,64,128]{3,2,1,0:T(8,128)S(1)} %get-tuple-element.29), channel_id=1, source_target_pairs={{0,1},{1,0},{2,3},{3,2},{4,5},{5,4},{6,7},{7,6},{8,9},{9,8},{10,11... | collective-permute-start | bytes 3145736 | tf_op jit(solution)/shard_map/ppermute | solution.py:336
  92.5 3.8 %shard_map.49.coef = f32[3,24,64,128]{3,2,1,0:T(8,128)} custom-call(s32[3]{0:T(128)} %pad_add_fusion.flags, f32[3,8,64,128]{3,2,1,0:T(8,128)} %shard_map.48.own, f32[3,8,64,128]{3,2,1,0:T(8,128)} %collective-permute-done.3.core, f32[3,8,64,128]{3,2,1,0:T(8,128)} %collective-permute-done.4.link), custom_call_target="tpu_custom_call" | custom-call | flops 4718592 | bytes 4718592 | tf_op jit(solution)/shard_map/pallas_call | solution.py:99
  96.3 12.3 %shard_map.50 = (f32[4,8,64,128]{3,2,1,0:T(8,128)}, f32[1,8,64,128]{3,2,1,0:T(8,128)}) custom-call(s32[3]{0:T(128)} %pad_add_fusion.flags, f32[3,8,64,128]{3,2,1,0:T(8,128)} %shard_map.48.own, f32[3,8,64,128]{3,2,1,0:T(8,128)} %collective-permute-done.3.core, f32[3,8,64,128]{3,2,1,0:T(8,128)} %collective-permute-done.4.link, f32[8,8,64,128]{3,2,1,0:T(8,128)} %copy-done, ...), custom_call_target="tpu_custom_call" | custom-call | flops 20971520 | bytes 10223616 | tf_op jit(solution)/shard_map/pallas_call | solution.py:99
  109.3 9.4 %collective-permute-start.7 = (f32[1,8,64,128]{3,2,1,0:T(8,128)}, f32[1,8,64,128]{3,2,1,0:T(8,128)}, u32[]{:S(2)}, u32[]{:S(2)}) collective-permute-start(f32[1,8,64,128]{3,2,1,0:T(8,128)} %get-tuple-element.23.own), channel_id=1, source_target_pairs={{0,1},{1,0},{2,3},{3,2},{4,5},{5,4},{6,7},{7,6},{8,9},{9,8},{10,11... | collective-permute-start | bytes 786440 | tf_op jit(solution)/shard_map/ppermute | solution.py:336
  120.2 12.5 %shard_map.51 = (f32[8,8,64,128]{3,2,1,0:T(8,128)}, f32[1,8,64,128]{3,2,1,0:T(8,128)}) custom-call(s32[3]{0:T(128)} %pad_add_fusion.flags, f32[1,8,64,128]{3,2,1,0:T(8,128)} %get-tuple-element.23.own, f32[1,8,64,128]{3,2,1,0:T(8,128)} %collective-permute-done.7.core, f32[1,8,64,128]{3,2,1,0:T(8,128)} %copy-done.10, f32[8,8,64,128]{3,2,1,0:T(8,128)} %copy-done, ...), custom_call_target="tpu_custom_call" | custom-call | flops 20971520 | bytes 10747904 | tf_op jit(solution)/shard_map/pallas_call | solution.py:99
  134.1 4.2 %collective-permute-done.11 = f32[1,8,64,128]{3,2,1,0:T(8,128)S(1)} collective-permute-done((f32[1,8,64,128]{3,2,1,0:T(8,128)}, f32[1,8,64,128]{3,2,1,0:T(8,128)S(1)}, u32[]{:S(2)}, u32[]{:S(2)}) %collective-permute-start.11) | collective-permute-done | bytes 262176 | tf_op jit(solution)/shard_map/ppermute | solution.py:398
  140.0 5.1 %collective-permute-start.12 = (f32[1,8,64,128]{3,2,1,0:T(8,128)S(1)}, f32[1,8,64,128]{3,2,1,0:T(8,128)S(1)}, u32[]{:S(2)}, u32[]{:S(2)}) collective-permute-start(f32[1,8,64,128]{3,2,1,0:T(8,128)S(1)} %slice_select_fusion.own), channel_id=1, source_target_pairs={{0,1},{1,0},{2,3},{3,2},{4,5},{5,4},{6,7},{7,6},{8,9},{9,8},{10,11... | collective-permute-start | bytes 786440 | tf_op jit(solution)/shard_map/ppermute | solution.py:336
  146.9 11.8 %shard_map.52 = (f32[4,8,64,128]{3,2,1,0:T(8,128)}, f32[1,8,64,128]{3,2,1,0:T(8,128)}) custom-call(s32[3]{0:T(128)} %pad_add_fusion.flags, f32[1,8,64,128]{3,2,1,0:T(8,128)} %copy-done.6, f32[1,8,64,128]{3,2,1,0:T(8,128)} %copy-done.14, f32[1,8,64,128]{3,2,1,0:T(8,128)} %copy-done.13, f32[8,8,64,128]{3,2,1,0:T(8,128)} %copy-done, ...), custom_call_target="tpu_custom_call" | custom-call | flops 20971520 | bytes 8650752 | tf_op jit(solution)/shard_map/pallas_call | solution.py:99
  159.6 7.0 %collective-permute-start.14 = (f32[1,8,64,128]{3,2,1,0:T(8,128)}, f32[1,8,64,128]{3,2,1,0:T(8,128)S(1)}, u32[]{:S(2)}, u32[]{:S(2)}) collective-permute-start(f32[1,8,64,128]{3,2,1,0:T(8,128)} %get-tuple-element.26.own), channel_id=1, source_target_pairs={{0,1},{1,0},{2,3},{3,2},{4,5},{5,4},{6,7},{7,6},{8,9},{9,8},{10,11... | collective-permute-start | bytes 786440 | tf_op jit(solution)/shard_map/ppermute | solution.py:336
  168.7 12.5 %shard_map.53 = (f32[8,8,64,128]{3,2,1,0:T(8,128)}, f32[1,8,64,128]{3,2,1,0:T(8,128)}) custom-call(s32[3]{0:T(128)} %pad_add_fusion.flags, f32[1,8,64,128]{3,2,1,0:T(8,128)} %get-tuple-element.26.own, f32[1,8,64,128]{3,2,1,0:T(8,128)} %copy-done.12, f32[1,8,64,128]{3,2,1,0:T(8,128)} %copy-done.11, f32[8,8,64,128]{3,2,1,0:T(8,128)} %copy-done, ...), custom_call_target="tpu_custom_call" | custom-call | flops 20971520 | bytes 10747904 | tf_op jit(solution)/shard_map/pallas_call | solution.py:99
  181.2 16.8 %all-to-all-start.2 = ((f32[8,8,64,128]{3,2,1,0:T(8,128)}), f32[8,8,64,128]{3,2,1,0:T(8,128)S(1)}, u32[]{:S(2)}, u32[]{:S(2)}) async-start(f32[8,8,64,128]{3,2,1,0:T(8,128)} %get-tuple-element.28), calls=%async_computation.2 | async-start | bytes 4194304 | tf_op jit(solution)/shard_map/all_to_all | solution.py:347
  197.9 24.4 %all-to-all-done.2 = f32[8,8,64,128]{3,2,1,0:T(8,128)S(1)} async-done(((f32[8,8,64,128]{3,2,1,0:T(8,128)}), f32[8,8,64,128]{3,2,1,0:T(8,128)S(1)}, u32[]{:S(2)}, u32[]{:S(2)}) %all-to-all-start.2) | async-done | bytes 2097184 | tf_op jit(solution)/shard_map/all_to_all | solution.py:347
  222.4 2.6 %collective-permute-done.16 = f32[4,8,64,128]{3,2,1,0:T(8,128)S(1)} collective-permute-done((f32[4,8,64,128]{3,2,1,0:T(8,128)S(1)}, f32[4,8,64,128]{3,2,1,0:T(8,128)S(1)}, u32[]{:S(2)}, u32[]{:S(2)}) %collective-permute-start.16) | collective-permute-done | bytes 1048608 | tf_op jit(solution)/shard_map/ppermute | solution.py:402
  226.1 5.6 %shard_map.54 = f32[64,64,128]{2,1,0:T(8,128)} custom-call(s32[3]{0:T(128)} %pad_add_fusion.flags, f32[4096,128]{1,0:T(8,128)} %bitcast.16, f32[2048,128]{1,0:T(8,128)} %bitcast.20), custom_call_target="tpu_custom_call" | custom-call | flops 5242880 | bytes 5242880 | tf_op jit(solution)/shard_map/pallas_call | solution.py:99
  (64 shorter events, 19.5 us)
Async XLA Ops:
  6.6 3.0 %collective-permute-start.2 = (f32[2048,128]{1,0:T(8,128)}, f32[2048,128]{1,0:T(8,128)S(1)}, u32[]{:S(2)}, u32[]{:S(2)}) collective-permute-start(f32[2048,128]{1,0:T(8,128)} %get-tuple-element.20), channel_id=1, source_target_pairs={{0,1},{1,0},{2,3},{3,2},{4,5},{5,4},{6,7},{7,6},{8,9},{9,8},{10,11... | collective-permute-start | bytes 3145736 | tf_op jit(solution)/shard_map/ppermute | solution.py:342
  10.6 6.2 %copy-start.7 = (f32[4,64,128]{2,1,0:T(8,128)S(1)}, f32[4,64,128]{2,1,0:T(8,128)}, u32[]{:S(2)}) copy-start(f32[4,64,128]{2,1,0:T(8,128)} %param.7) | copy-start | bytes 393220
  10.6 6.2 %copy-start.8 = (f32[4,64,128]{2,1,0:T(8,128)S(1)}, f32[4,64,128]{2,1,0:T(8,128)}, u32[]{:S(2)}) copy-start(f32[4,64,128]{2,1,0:T(8,128)} %param.6) | copy-start | bytes 393220
  10.6 6.3 %copy-start.9 = (f32[4,64,128]{2,1,0:T(8,128)S(1)}, f32[4,64,128]{2,1,0:T(8,128)}, u32[]{:S(2)}) copy-start(f32[4,64,128]{2,1,0:T(8,128)} %param.5) | copy-start | bytes 393220
  10.6 44.5 %all-to-all-start = ((f32[8,8,64,128]{3,2,1,0:T(8,128)}), f32[8,8,64,128]{3,2,1,0:T(8,128)S(1)}, u32[]{:S(2)}, u32[]{:S(2)}) async-start(f32[8,8,64,128]{3,2,1,0:T(8,128)} %bitcast.19), calls=%async_computation | async-start | bytes 4194304 | tf_op jit(solution)/shard_map/all_to_all | solution.py:347
  16.9 31.4 %collective-permute-start = (f32[3,4,64,128]{3,2,1,0:T(8,128)S(1)}, f32[3,4,64,128]{3,2,1,0:T(8,128)S(1)}, u32[]{:S(2)}, u32[]{:S(2)}) collective-permute-start(f32[3,4,64,128]{3,2,1,0:T(8,128)S(1)} %pad_maximum_fusion.1), channel_id=1, source_target_pairs={{0,16},{2,18},{4,20},{6,22},{8,24},{10,26},{12,28},{14,30},{16,0},... | collective-permute-start | bytes 1179656 | tf_op jit(solution)/shard_map/ppermute | solution.py:350
  52.4 1.9 collective-permute-start.1
  55.1 28.6 %copy-start = (f32[8,8,64,128]{3,2,1,0:T(8,128)}, f32[8,8,64,128]{3,2,1,0:T(8,128)S(1)}, u32[]{:S(2)}) copy-start(f32[8,8,64,128]{3,2,1,0:T(8,128)S(1)} %all-to-all-done.f_own) | copy-start | bytes 6291460
  80.9 5.9 %collective-permute-start.4 = (f32[3,8,64,128]{3,2,1,0:T(8,128)}, f32[3,8,64,128]{3,2,1,0:T(8,128)}, u32[]{:S(2)}, u32[]{:S(2)}) collective-permute-start(f32[3,8,64,128]{3,2,1,0:T(8,128)} %shard_map.48.own), channel_id=1, source_target_pairs={{1,3},{3,1},{17,19},{19,17},{2,6},{6,2},{18,22},{22,18},{7,5},{5,7... | collective-permute-start | bytes 2359304 | tf_op jit(solution)/shard_map/ppermute | solution.py:336
  83.7 12.6 %collective-permute-start.6 = (f32[4,8,64,128]{3,2,1,0:T(8,128)}, f32[4,8,64,128]{3,2,1,0:T(8,128)}, u32[]{:S(2)}, u32[]{:S(2)}) collective-permute-start(f32[4,8,64,128]{3,2,1,0:T(8,128)} %get-tuple-element.30), channel_id=1, source_target_pairs={{1,3},{3,1},{17,19},{19,17},{2,6},{6,2},{18,22},{22,18},{7,5},{5,7... | collective-permute-start | bytes 3145736 | tf_op jit(solution)/shard_map/ppermute | solution.py:336
  85.4 10.9 %collective-permute-start.5 = (f32[4,8,64,128]{3,2,1,0:T(8,128)}, f32[4,8,64,128]{3,2,1,0:T(8,128)}, u32[]{:S(2)}, u32[]{:S(2)}) collective-permute-start(f32[4,8,64,128]{3,2,1,0:T(8,128)} %get-tuple-element.30), channel_id=1, source_target_pairs={{0,1},{1,0},{2,3},{3,2},{4,5},{5,4},{6,7},{7,6},{8,9},{9,8},{10,11... | collective-permute-start | bytes 3145736 | tf_op jit(solution)/shard_map/ppermute | solution.py:336
  86.0 6.5 %collective-permute-start.3 = (f32[3,8,64,128]{3,2,1,0:T(8,128)S(1)}, f32[3,8,64,128]{3,2,1,0:T(8,128)}, u32[]{:S(2)}, u32[]{:S(2)}) collective-permute-start(f32[3,8,64,128]{3,2,1,0:T(8,128)S(1)} %copy-done.2), channel_id=1, source_target_pairs={{0,1},{1,0},{2,3},{3,2},{4,5},{5,4},{6,7},{7,6},{8,9},{9,8},{10,11... | collective-permute-start | bytes 2359304 | tf_op jit(solution)/shard_map/ppermute | solution.py:336
  86.1 32.6 %collective-permute-start.10 = (f32[4,8,64,128]{3,2,1,0:T(8,128)S(1)}, f32[4,8,64,128]{3,2,1,0:T(8,128)S(1)}, u32[]{:S(2)}, u32[]{:S(2)}) collective-permute-start(f32[4,8,64,128]{3,2,1,0:T(8,128)S(1)} %get-tuple-element.29), channel_id=1, source_target_pairs={{1,3},{3,1},{17,19},{19,17},{2,6},{6,2},{18,22},{22,18},{7,5},{5,7... | collective-permute-start | bytes 3145736 | tf_op jit(solution)/shard_map/ppermute | solution.py:336
  86.8 31.9 %collective-permute-start.9 = (f32[4,8,64,128]{3,2,1,0:T(8,128)S(1)}, f32[4,8,64,128]{3,2,1,0:T(8,128)S(1)}, u32[]{:S(2)}, u32[]{:S(2)}) collective-permute-start(f32[4,8,64,128]{3,2,1,0:T(8,128)S(1)} %get-tuple-element.29), channel_id=1, source_target_pairs={{0,1},{1,0},{2,3},{3,2},{4,5},{5,4},{6,7},{7,6},{8,9},{9,8},{10,11... | collective-permute-start | bytes 3145736 | tf_op jit(solution)/shard_map/ppermute | solution.py:336
  108.6 10.1 %collective-permute-start.8 = (f32[1,8,64,128]{3,2,1,0:T(8,128)}, f32[1,8,64,128]{3,2,1,0:T(8,128)S(1)}, u32[]{:S(2)}, u32[]{:S(2)}) collective-permute-start(f32[1,8,64,128]{3,2,1,0:T(8,128)} %get-tuple-element.23.own), channel_id=1, source_target_pairs={{1,3},{3,1},{17,19},{19,17},{2,6},{6,2},{18,22},{22,18},{7,5},{5,7... | collective-permute-start | bytes 786440 | tf_op jit(solution)/shard_map/ppermute | solution.py:336
  109.3 10.9 %collective-permute-start.7 = (f32[1,8,64,128]{3,2,1,0:T(8,128)}, f32[1,8,64,128]{3,2,1,0:T(8,128)}, u32[]{:S(2)}, u32[]{:S(2)}) collective-permute-start(f32[1,8,64,128]{3,2,1,0:T(8,128)} %get-tuple-element.23.own), channel_id=1, source_target_pairs={{0,1},{1,0},{2,3},{3,2},{4,5},{5,4},{6,7},{7,6},{8,9},{9,8},{10,11... | collective-permute-start | bytes 786440 | tf_op jit(solution)/shard_map/ppermute | solution.py:336
  132.6 5.7 %collective-permute-start.11 = (f32[1,8,64,128]{3,2,1,0:T(8,128)}, f32[1,8,64,128]{3,2,1,0:T(8,128)S(1)}, u32[]{:S(2)}, u32[]{:S(2)}) collective-permute-start(f32[1,8,64,128]{3,2,1,0:T(8,128)} %get-tuple-element.25), channel_id=1, source_target_pairs={{0,16},{1,17},{2,18},{3,19},{4,20},{5,21},{6,22},{7,23},{8,24},{9,... | collective-permute-start | bytes 786440 | tf_op jit(solution)/shard_map/ppermute | solution.py:398
  139.3 6.9 %copy-start.6 = (f32[1,8,64,128]{3,2,1,0:T(8,128)}, f32[1,8,64,128]{3,2,1,0:T(8,128)S(1)}, u32[]{:S(2)}) copy-start(f32[1,8,64,128]{3,2,1,0:T(8,128)S(1)} %slice_select_fusion.own) | copy-start | bytes 786436
  139.3 5.7 %collective-permute-start.13 = (f32[1,8,64,128]{3,2,1,0:T(8,128)S(1)}, f32[1,8,64,128]{3,2,1,0:T(8,128)S(1)}, u32[]{:S(2)}, u32[]{:S(2)}) collective-permute-start(f32[1,8,64,128]{3,2,1,0:T(8,128)S(1)} %slice_select_fusion.own), channel_id=1, source_target_pairs={{1,3},{3,1},{17,19},{19,17},{2,6},{6,2},{18,22},{22,18},{7,5},{5,7... | collective-permute-start | bytes 786440 | tf_op jit(solution)/shard_map/ppermute | solution.py:336
  140.0 6.2 %collective-permute-start.12 = (f32[1,8,64,128]{3,2,1,0:T(8,128)S(1)}, f32[1,8,64,128]{3,2,1,0:T(8,128)S(1)}, u32[]{:S(2)}, u32[]{:S(2)}) collective-permute-start(f32[1,8,64,128]{3,2,1,0:T(8,128)S(1)} %slice_select_fusion.own), channel_id=1, source_target_pairs={{0,1},{1,0},{2,3},{3,2},{4,5},{5,4},{6,7},{7,6},{8,9},{9,8},{10,11... | collective-permute-start | bytes 786440 | tf_op jit(solution)/shard_map/ppermute | solution.py:336
  158.7 7.9 %collective-permute-start.15 = (f32[1,8,64,128]{3,2,1,0:T(8,128)}, f32[1,8,64,128]{3,2,1,0:T(8,128)S(1)}, u32[]{:S(2)}, u32[]{:S(2)}) collective-permute-start(f32[1,8,64,128]{3,2,1,0:T(8,128)} %get-tuple-element.26.own), channel_id=1, source_target_pairs={{1,3},{3,1},{17,19},{19,17},{2,6},{6,2},{18,22},{22,18},{7,5},{5,7... | collective-permute-start | bytes 786440 | tf_op jit(solution)/shard_map/ppermute | solution.py:336
  159.6 8.4 %collective-permute-start.14 = (f32[1,8,64,128]{3,2,1,0:T(8,128)}, f32[1,8,64,128]{3,2,1,0:T(8,128)S(1)}, u32[]{:S(2)}, u32[]{:S(2)}) collective-permute-start(f32[1,8,64,128]{3,2,1,0:T(8,128)} %get-tuple-element.26.own), channel_id=1, source_target_pairs={{0,1},{1,0},{2,3},{3,2},{4,5},{5,4},{6,7},{7,6},{8,9},{9,8},{10,11... | collective-permute-start | bytes 786440 | tf_op jit(solution)/shard_map/ppermute | solution.py:336
  181.2 41.1 %all-to-all-start.2 = ((f32[8,8,64,128]{3,2,1,0:T(8,128)}), f32[8,8,64,128]{3,2,1,0:T(8,128)S(1)}, u32[]{:S(2)}, u32[]{:S(2)}) async-start(f32[8,8,64,128]{3,2,1,0:T(8,128)} %get-tuple-element.28), calls=%async_computation.2 | async-start | bytes 4194304 | tf_op jit(solution)/shard_map/all_to_all | solution.py:347
  222.4 2.7 %collective-permute-start.16 = (f32[4,8,64,128]{3,2,1,0:T(8,128)S(1)}, f32[4,8,64,128]{3,2,1,0:T(8,128)S(1)}, u32[]{:S(2)}, u32[]{:S(2)}) collective-permute-start(f32[4,8,64,128]{3,2,1,0:T(8,128)S(1)} %constant_dynamic-slice_fusion), channel_id=1, source_target_pairs={{0,1},{1,0},{2,3},{3,2},{4,5},{5,4},{6,7},{7,6},{8,9},{9,8},{10,11... | collective-permute-start | bytes 3145736 | tf_op jit(solution)/shard_map/ppermute | solution.py:402
  (10 other events, 17.3 us)

commit v3 on v2

--- a/solution.py
+++ b/solution.py
@@ -15,6 +15,7 @@
 ROWS = 8
 FILL = 4
 BATCH = 24
+VMEM = 24 << 20
 
 
 def padded(shard, sides, width):
@@ -104,6 +105,7 @@
         out_specs=jax.tree.map(lambda _: pl.BlockSpec(memory_space=pltpu.VMEM), out_shape),
         scratch_shapes=list(scratch),
         cost_estimate=pl.CostEstimate(flops=flops or size, bytes_accessed=size, transcendentals=0),
+        compiler_params=pltpu.CompilerParams(vmem_limit_bytes=VMEM),
     )(flags, *operands)
 
 
@@ -268,7 +270,7 @@
     va[ghost, inside] = swap_lanes(va[planes, inside])
 
     def relax(src, dst, first):
-        cells = [(z, i) for z in range(0, zrows, ROWS) for i in reversed(range(first, planes))]
+        cells = [(z, i) for i in reversed(range(first, planes)) for z in range(0, zrows, ROWS)]
         for lead in range(0, len(cells), BATCH):
             part = cells[lead : lead + BATCH]
             field = [src[1 + i, ROWS + z : 2 * ROWS + z] for z, i in part]
@@ -363,7 +365,9 @@
     near = exchange(fields)
     region = jax.ShapeDtypeStruct((3, 3 * ROWS, zlen, LANES), f32)
     coef = call(prep_kernel, region, (fields, *near), flags)
-    halos = [exchange(force[k : k + spw]) for k in range(0, chips, spw)]
+    halos = []
+    for k in range(0, chips, spw):
+        halos.append(exchange(force[k : k + spw]))
 
     wide = pltpu.VMEM((3 * ROWS + 2, zlen + 2 * ROWS, LANES), f32)
     scratch = (

time: 232 us -> 208 us (0.90)
  Pallas kernels: 69.6 us -> 45.5 us
    pallas_call x9, Pallas kernels: 69.6 us -> 45.5 us  [call(): pl.pallas_call(kernel, grid=grid, out_shape=out_shape, in_specs=[pl.Block...]
  transfers between devices with their start and end apart: 19 -> 19, of which waited for: 9 -> 9; matrix products, arithmetic and copies ran while one was open for 1% -> 1% of each run, Pallas kernels for 8% -> 5%
where the time goes in v3:
time: 208 us
  waiting for transfers between devices  68.2 us (33%)
  starting transfers between devices  63.2 us (30%)
  Pallas kernels  45.5 us (22%)
  blocking collectives  23.3 us (11%)
  local copies, waits for them, and re-layouts  6.81 us (3%)
    pallas_call x9, Pallas kernels, call(): pl.pallas_call(kernel, grid=grid, out_shape=out_shape, in_specs=[pl.Block...  45.5 us
    ppermute x12, starting transfers between devices, exchange(): return (lax.ppermute(x, 'space', cores), lax.ppermute(x, both, across))  36.1 us
    ppermute x1, waiting for transfers between devices, split_along_y(): lax.ppermute(fields, 'tm', [(i, (i + chips) % (2 * chips)) for i in range...  28.8 us
    all_to_all x2, waiting for transfers between devices, to_chips(): return lax.all_to_all(x, 'tm', 0, 0, axis_index_groups=groups, tiled=True)  24.6 us
    all_to_all x1, blocking collectives, to_chips(): return lax.all_to_all(x, 'tm', 0, 0, axis_index_groups=groups, tiled=True)  23.3 us
    all_to_all x2, starting transfers between devices, to_chips(): return lax.all_to_all(x, 'tm', 0, 0, axis_index_groups=groups, tiled=True)  22.4 us
    ppermute x2, waiting for transfers between devices, packed(): got = lax.ppermute(send, 'space', cores)  4.47 us
    unnamed x12, local copies, waits for them, and re-layouts  4.23 us
  transfers between devices with their start and end apart: 19, of which 9 were waited for; matrix products, arithmetic and copies ran while one was open for 1% of the time, Pallas kernels for 5%

profile of v3, /device:TPU:0, one launch (start us, length us, event | category | flops | bytes accessed | tf_op | source)
XLA Modules:
  0.0 207.5 jit_solution(7299286261071462598)
XLA Ops:
  0.1 1.6 copy-done
  1.7 4.1 %shard_map.47 = (f32[4096,128]{1,0:T(8,128)S(1)}, f32[2048,128]{1,0:T(8,128)}) custom-call(s32[3]{0:T(128)S(1)} %pad_add_fusion.flags, f32[64,64,128]{2,1,0:T(8,128)S(1)} %bitcast.18), custom_call_target="tpu_custom_call" | custom-call | flops 5242880 | bytes 5242880 | tf_op jit(solution)/shard_map/pallas_call | solution.py:100
  6.3 2.6 %collective-permute-done.2 = f32[2048,128]{1,0:T(8,128)} collective-permute-done((f32[2048,128]{1,0:T(8,128)}, f32[2048,128]{1,0:T(8,128)}, u32[]{:S(2)}, u32[]{:S(2)}) %collective-permute-start.2) | collective-permute-done | bytes 1048608 | tf_op jit(solution)/shard_map/ppermute | solution.py:344
  11.5 6.2 %all-to-all-start = ((f32[8,8,64,128]{3,2,1,0:T(8,128)}), f32[8,8,64,128]{3,2,1,0:T(8,128)S(1)}, u32[]{:S(2)}, u32[]{:S(2)}) async-start(f32[8,8,64,128]{3,2,1,0:T(8,128)} %bitcast.19), calls=%async_computation | async-start | bytes 4194304 | tf_op jit(solution)/shard_map/all_to_all | solution.py:349
  17.8 2.7 %collective-permute-start = (f32[3,4,64,128]{3,2,1,0:T(8,128)S(1)}, f32[3,4,64,128]{3,2,1,0:T(8,128)S(1)}, u32[]{:S(2)}, u32[]{:S(2)}) collective-permute-start(f32[3,4,64,128]{3,2,1,0:T(8,128)S(1)} %pad_maximum_fusion.1), channel_id=1, source_target_pairs={{0,16},{2,18},{4,20},{6,22},{8,24},{10,26},{12,28},{14,30},{16,0},... | collective-permute-start | bytes 1179656 | tf_op jit(solution)/shard_map/ppermute | solution.py:352
  20.5 28.8 %collective-permute-done = f32[3,4,64,128]{3,2,1,0:T(8,128)S(1)} collective-permute-done((f32[3,4,64,128]{3,2,1,0:T(8,128)S(1)}, f32[3,4,64,128]{3,2,1,0:T(8,128)S(1)}, u32[]{:S(2)}, u32[]{:S(2)}) %collective-permute-start) | collective-permute-done | bytes 393248 | tf_op jit(solution)/shard_map/ppermute | solution.py:352
  49.5 1.3 shard_map.46
  50.9 1.8 collective-permute-done.1
  53.8 23.3 %all_to_all.15.got = f32[8,8,24,128]{3,2,1,0:T(8,128)S(1)} all-to-all(f32[8,8,24,128]{3,2,1,0:T(8,128)S(1)} %bitcast.21), channel_id=1, replica_groups={{0,2,4,6,8,10,12,14},{16,18,20,22,24,26,28,30},{1,3,5,7,9,11,13,15},{17..., dimensions={0} | all-to-all | bytes 1572864 | tf_op jit(solution)/shard_map/all_to_all | solution.py:349
  79.4 2.4 %collective-permute-start.5 = (f32[4,8,64,128]{3,2,1,0:T(8,128)S(1)}, f32[4,8,64,128]{3,2,1,0:T(8,128)S(1)}, u32[]{:S(2)}, u32[]{:S(2)}) collective-permute-start(f32[4,8,64,128]{3,2,1,0:T(8,128)S(1)} %get-tuple-element.30), channel_id=1, source_target_pairs={{0,1},{1,0},{2,3},{3,2},{4,5},{5,4},{6,7},{7,6},{8,9},{9,8},{10,11... | collective-permute-start | bytes 3145736 | tf_op jit(solution)/shard_map/ppermute | solution.py:338
  82.6 6.4 %collective-permute-start.9 = (f32[4,8,64,128]{3,2,1,0:T(8,128)S(1)}, f32[4,8,64,128]{3,2,1,0:T(8,128)S(1)}, u32[]{:S(2)}, u32[]{:S(2)}) collective-permute-start(f32[4,8,64,128]{3,2,1,0:T(8,128)S(1)} %get-tuple-element.29), channel_id=1, source_target_pairs={{0,1},{1,0},{2,3},{3,2},{4,5},{5,4},{6,7},{7,6},{8,9},{9,8},{10,11... | collective-permute-start | bytes 3145736 | tf_op jit(solution)/shard_map/ppermute | solution.py:338
  90.3 7.9 %shard_map.50 = (f32[4,8,64,128]{3,2,1,0:T(8,128)S(1)}, f32[1,8,64,128]{3,2,1,0:T(8,128)S(1)}) custom-call(s32[3]{0:T(128)S(1)} %pad_add_fusion.flags, f32[3,8,64,128]{3,2,1,0:T(8,128)S(1)} %shard_map.48.own, f32[3,8,64,128]{3,2,1,0:T(8,128)S(1)} %collective-permute-done.3.core, f32[3,8,64,128]{3,2,1,0:T(8,128)S(1)} %collective-permute-done.4.link, ...), custom_call_target="tpu_custom_call" | custom-call | flops 20971520 | bytes 10223616 | tf_op jit(solution)/shard_map/pallas_call | solution.py:100
  98.9 11.8 %collective-permute-start.7 = (f32[1,8,64,128]{3,2,1,0:T(8,128)S(1)}, f32[1,8,64,128]{3,2,1,0:T(8,128)S(1)}, u32[]{:S(2)}, u32[]{:S(2)}) collective-permute-start(f32[1,8,64,128]{3,2,1,0:T(8,128)S(1)} %get-tuple-element.23.own), channel_id=1, source_target_pairs={{0,1},{1,0},{2,3},{3,2},{4,5},{5,4},{6,7},{7,6},{8,9},{9,8},{10,11... | collective-permute-start | bytes 786440 | tf_op jit(solution)/shard_map/ppermute | solution.py:338
  111.9 9.3 %shard_map.51 = (f32[8,8,64,128]{3,2,1,0:T(8,128)}, f32[1,8,64,128]{3,2,1,0:T(8,128)S(1)}) custom-call(s32[3]{0:T(128)S(1)} %pad_add_fusion.flags, f32[1,8,64,128]{3,2,1,0:T(8,128)S(1)} %get-tuple-element.23.own, f32[1,8,64,128]{3,2,1,0:T(8,128)S(1)} %collective-permute-done.7.core, f32[1,8,64,128]{3,2,1,0:T(8,128)S(1)} %collective-permute-done.8.link, ...), custom_call_target="tpu_custom_call" | custom-call | flops 20971520 | bytes 10747904 | tf_op jit(solution)/shard_map/pallas_call | solution.py:100
  121.2 1.5 collective-permute-start.11
  122.6 4.2 %collective-permute-done.11 = f32[1,8,64,128]{3,2,1,0:T(8,128)S(1)} collective-permute-done((f32[1,8,64,128]{3,2,1,0:T(8,128)S(1)}, f32[1,8,64,128]{3,2,1,0:T(8,128)S(1)}, u32[]{:S(2)}, u32[]{:S(2)}) %collective-permute-start.11) | collective-permute-done | bytes 262176 | tf_op jit(solution)/shard_map/ppermute | solution.py:402
  127.5 4.2 %collective-permute-start.12 = (f32[1,8,64,128]{3,2,1,0:T(8,128)S(1)}, f32[1,8,64,128]{3,2,1,0:T(8,128)S(1)}, u32[]{:S(2)}, u32[]{:S(2)}) collective-permute-start(f32[1,8,64,128]{3,2,1,0:T(8,128)S(1)} %slice_select_fusion.own), channel_id=1, source_target_pairs={{0,1},{1,0},{2,3},{3,2},{4,5},{5,4},{6,7},{7,6},{8,9},{9,8},{10,11... | collective-permute-start | bytes 786440 | tf_op jit(solution)/shard_map/ppermute | solution.py:338
  132.9 7.9 %shard_map.52 = (f32[4,8,64,128]{3,2,1,0:T(8,128)S(1)}, f32[1,8,64,128]{3,2,1,0:T(8,128)S(1)}) custom-call(s32[3]{0:T(128)S(1)} %pad_add_fusion.flags, f32[1,8,64,128]{3,2,1,0:T(8,128)S(1)} %slice_select_fusion.own, f32[1,8,64,128]{3,2,1,0:T(8,128)S(1)} %collective-permute-done.12.core, f32[1,8,64,128]{3,2,1,0:T(8,128)S(1)} %collective-permute-done.13.link, ...), custom_call_target="tpu_custom_call" | custom-call | flops 20971520 | bytes 8650752 | tf_op jit(solution)/shard_map/pallas_call | solution.py:100
  141.5 7.0 %collective-permute-start.14 = (f32[1,8,64,128]{3,2,1,0:T(8,128)S(1)}, f32[1,8,64,128]{3,2,1,0:T(8,128)S(1)}, u32[]{:S(2)}, u32[]{:S(2)}) collective-permute-start(f32[1,8,64,128]{3,2,1,0:T(8,128)S(1)} %get-tuple-element.26.own), channel_id=1, source_target_pairs={{0,1},{1,0},{2,3},{3,2},{4,5},{5,4},{6,7},{7,6},{8,9},{9,8},{10,11... | collective-permute-start | bytes 786440 | tf_op jit(solution)/shard_map/ppermute | solution.py:338
  149.7 8.7 %shard_map.53 = (f32[8,8,64,128]{3,2,1,0:T(8,128)S(1)}, f32[1,8,64,128]{3,2,1,0:T(8,128)}) custom-call(s32[3]{0:T(128)S(1)} %pad_add_fusion.flags, f32[1,8,64,128]{3,2,1,0:T(8,128)S(1)} %get-tuple-element.26.own, f32[1,8,64,128]{3,2,1,0:T(8,128)S(1)} %collective-permute-done.14.core, f32[1,8,64,128]{3,2,1,0:T(8,128)S(1)} %collective-permute-done.15.link, ...), custom_call_target="tpu_custom_call" | custom-call | flops 20971520 | bytes 10747904 | tf_op jit(solution)/shard_map/pallas_call | solution.py:100
  159.7 16.2 %all-to-all-start.2 = ((f32[8,8,64,128]{3,2,1,0:T(8,128)}), f32[8,8,64,128]{3,2,1,0:T(8,128)S(1)}, u32[]{:S(2)}, u32[]{:S(2)}) async-start(f32[8,8,64,128]{3,2,1,0:T(8,128)} %copy-done.1), calls=%async_computation.2 | async-start | bytes 4194304 | tf_op jit(solution)/shard_map/all_to_all | solution.py:349
  175.8 24.6 %all-to-all-done.2 = f32[8,8,64,128]{3,2,1,0:T(8,128)S(1)} async-done(((f32[8,8,64,128]{3,2,1,0:T(8,128)}), f32[8,8,64,128]{3,2,1,0:T(8,128)S(1)}, u32[]{:S(2)}, u32[]{:S(2)}) %all-to-all-start.2) | async-done | bytes 2097184 | tf_op jit(solution)/shard_map/all_to_all | solution.py:349
  200.6 2.6 %collective-permute-done.16 = f32[4,8,64,128]{3,2,1,0:T(8,128)S(1)} collective-permute-done((f32[4,8,64,128]{3,2,1,0:T(8,128)S(1)}, f32[4,8,64,128]{3,2,1,0:T(8,128)S(1)}, u32[]{:S(2)}, u32[]{:S(2)}) %collective-permute-start.16) | collective-permute-done | bytes 1048608 | tf_op jit(solution)/shard_map/ppermute | solution.py:406
  203.3 4.3 %shard_map.54 = f32[64,64,128]{2,1,0:T(8,128)} custom-call(s32[3]{0:T(128)S(1)} %pad_add_fusion.flags, f32[4096,128]{1,0:T(8,128)S(1)} %bitcast.16, f32[2048,128]{1,0:T(8,128)S(1)} %bitcast.20), custom_call_target="tpu_custom_call" | custom-call | flops 5242880 | bytes 5242880 | tf_op jit(solution)/shard_map/pallas_call | solution.py:100
  (46 shorter events, 15.9 us)
Async XLA Ops:
  0.1 1.6 copy-start
  5.8 3.1 %collective-permute-start.2 = (f32[2048,128]{1,0:T(8,128)}, f32[2048,128]{1,0:T(8,128)}, u32[]{:S(2)}, u32[]{:S(2)}) collective-permute-start(f32[2048,128]{1,0:T(8,128)} %get-tuple-element.20), channel_id=1, source_target_pairs={{0,1},{1,0},{2,3},{3,2},{4,5},{5,4},{6,7},{7,6},{8,9},{9,8},{10,11... | collective-permute-start | bytes 3145736 | tf_op jit(solution)/shard_map/ppermute | solution.py:344
  10.2 1.3 copy-start.2
  11.5 6.2 %copy-start.3 = (f32[4,64,128]{2,1,0:T(8,128)S(1)}, f32[4,64,128]{2,1,0:T(8,128)}, u32[]{:S(2)}) copy-start(f32[4,64,128]{2,1,0:T(8,128)} %param.7) | copy-start | bytes 393220
  11.5 6.2 %copy-start.4 = (f32[4,64,128]{2,1,0:T(8,128)S(1)}, f32[4,64,128]{2,1,0:T(8,128)}, u32[]{:S(2)}) copy-start(f32[4,64,128]{2,1,0:T(8,128)} %param.6) | copy-start | bytes 393220
  11.5 6.3 %copy-start.5 = (f32[4,64,128]{2,1,0:T(8,128)S(1)}, f32[4,64,128]{2,1,0:T(8,128)}, u32[]{:S(2)}) copy-start(f32[4,64,128]{2,1,0:T(8,128)} %param.5) | copy-start | bytes 393220
  11.5 42.2 %all-to-all-start = ((f32[8,8,64,128]{3,2,1,0:T(8,128)}), f32[8,8,64,128]{3,2,1,0:T(8,128)S(1)}, u32[]{:S(2)}, u32[]{:S(2)}) async-start(f32[8,8,64,128]{3,2,1,0:T(8,128)} %bitcast.19), calls=%async_computation | async-start | bytes 4194304 | tf_op jit(solution)/shard_map/all_to_all | solution.py:349
  17.8 31.4 %collective-permute-start = (f32[3,4,64,128]{3,2,1,0:T(8,128)S(1)}, f32[3,4,64,128]{3,2,1,0:T(8,128)S(1)}, u32[]{:S(2)}, u32[]{:S(2)}) collective-permute-start(f32[3,4,64,128]{3,2,1,0:T(8,128)S(1)} %pad_maximum_fusion.1), channel_id=1, source_target_pairs={{0,16},{2,18},{4,20},{6,22},{8,24},{10,26},{12,28},{14,30},{16,0},... | collective-permute-start | bytes 1179656 | tf_op jit(solution)/shard_map/ppermute | solution.py:352
  50.8 1.9 collective-permute-start.1
  77.8 4.8 %collective-permute-start.4 = (f32[3,8,64,128]{3,2,1,0:T(8,128)S(1)}, f32[3,8,64,128]{3,2,1,0:T(8,128)S(1)}, u32[]{:S(2)}, u32[]{:S(2)}) collective-permute-start(f32[3,8,64,128]{3,2,1,0:T(8,128)S(1)} %shard_map.48.own), channel_id=1, source_target_pairs={{1,3},{3,1},{17,19},{19,17},{2,6},{6,2},{18,22},{22,18},{7,5},{5,7... | collective-permute-start | bytes 2359304 | tf_op jit(solution)/shard_map/ppermute | solution.py:338
  78.7 11.6 %collective-permute-start.6 = (f32[4,8,64,128]{3,2,1,0:T(8,128)S(1)}, f32[4,8,64,128]{3,2,1,0:T(8,128)S(1)}, u32[]{:S(2)}, u32[]{:S(2)}) collective-permute-start(f32[4,8,64,128]{3,2,1,0:T(8,128)S(1)} %get-tuple-element.30), channel_id=1, source_target_pairs={{1,3},{3,1},{17,19},{19,17},{2,6},{6,2},{18,22},{22,18},{7,5},{5,7... | collective-permute-start | bytes 3145736 | tf_op jit(solution)/shard_map/ppermute | solution.py:338
  79.4 10.9 %collective-permute-start.5 = (f32[4,8,64,128]{3,2,1,0:T(8,128)S(1)}, f32[4,8,64,128]{3,2,1,0:T(8,128)S(1)}, u32[]{:S(2)}, u32[]{:S(2)}) collective-permute-start(f32[4,8,64,128]{3,2,1,0:T(8,128)S(1)} %get-tuple-element.30), channel_id=1, source_target_pairs={{0,1},{1,0},{2,3},{3,2},{4,5},{5,4},{6,7},{7,6},{8,9},{9,8},{10,11... | collective-permute-start | bytes 3145736 | tf_op jit(solution)/shard_map/ppermute | solution.py:338
  81.8 7.2 %collective-permute-start.3 = (f32[3,8,64,128]{3,2,1,0:T(8,128)S(1)}, f32[3,8,64,128]{3,2,1,0:T(8,128)S(1)}, u32[]{:S(2)}, u32[]{:S(2)}) collective-permute-start(f32[3,8,64,128]{3,2,1,0:T(8,128)S(1)} %shard_map.48.own), channel_id=1, source_target_pairs={{0,1},{1,0},{2,3},{3,2},{4,5},{5,4},{6,7},{7,6},{8,9},{9,8},{10,11... | collective-permute-start | bytes 2359304 | tf_op jit(solution)/shard_map/ppermute | solution.py:338
  81.9 28.9 %collective-permute-start.10 = (f32[4,8,64,128]{3,2,1,0:T(8,128)S(1)}, f32[4,8,64,128]{3,2,1,0:T(8,128)S(1)}, u32[]{:S(2)}, u32[]{:S(2)}) collective-permute-start(f32[4,8,64,128]{3,2,1,0:T(8,128)S(1)} %get-tuple-element.29), channel_id=1, source_target_pairs={{1,3},{3,1},{17,19},{19,17},{2,6},{6,2},{18,22},{22,18},{7,5},{5,7... | collective-permute-start | bytes 3145736 | tf_op jit(solution)/shard_map/ppermute | solution.py:338
  82.6 28.1 %collective-permute-start.9 = (f32[4,8,64,128]{3,2,1,0:T(8,128)S(1)}, f32[4,8,64,128]{3,2,1,0:T(8,128)S(1)}, u32[]{:S(2)}, u32[]{:S(2)}) collective-permute-start(f32[4,8,64,128]{3,2,1,0:T(8,128)S(1)} %get-tuple-element.29), channel_id=1, source_target_pairs={{0,1},{1,0},{2,3},{3,2},{4,5},{5,4},{6,7},{7,6},{8,9},{9,8},{10,11... | collective-permute-start | bytes 3145736 | tf_op jit(solution)/shard_map/ppermute | solution.py:338
  98.2 12.5 %collective-permute-start.8 = (f32[1,8,64,128]{3,2,1,0:T(8,128)S(1)}, f32[1,8,64,128]{3,2,1,0:T(8,128)S(1)}, u32[]{:S(2)}, u32[]{:S(2)}) collective-permute-start(f32[1,8,64,128]{3,2,1,0:T(8,128)S(1)} %get-tuple-element.23.own), channel_id=1, source_target_pairs={{1,3},{3,1},{17,19},{19,17},{2,6},{6,2},{18,22},{22,18},{7,5},{5,7... | collective-permute-start | bytes 786440 | tf_op jit(solution)/shard_map/ppermute | solution.py:338
  98.9 13.0 %collective-permute-start.7 = (f32[1,8,64,128]{3,2,1,0:T(8,128)S(1)}, f32[1,8,64,128]{3,2,1,0:T(8,128)S(1)}, u32[]{:S(2)}, u32[]{:S(2)}) collective-permute-start(f32[1,8,64,128]{3,2,1,0:T(8,128)S(1)} %get-tuple-element.23.own), channel_id=1, source_target_pairs={{0,1},{1,0},{2,3},{3,2},{4,5},{5,4},{6,7},{7,6},{8,9},{9,8},{10,11... | collective-permute-start | bytes 786440 | tf_op jit(solution)/shard_map/ppermute | solution.py:338
  121.2 5.6 %collective-permute-start.11 = (f32[1,8,64,128]{3,2,1,0:T(8,128)S(1)}, f32[1,8,64,128]{3,2,1,0:T(8,128)S(1)}, u32[]{:S(2)}, u32[]{:S(2)}) collective-permute-start(f32[1,8,64,128]{3,2,1,0:T(8,128)S(1)} %get-tuple-element.25), channel_id=1, source_target_pairs={{0,16},{1,17},{2,18},{3,19},{4,20},{5,21},{6,22},{7,23},{8,24},{9,... | collective-permute-start | bytes 786440 | tf_op jit(solution)/shard_map/ppermute | solution.py:402
  126.9 4.9 %collective-permute-start.13 = (f32[1,8,64,128]{3,2,1,0:T(8,128)S(1)}, f32[1,8,64,128]{3,2,1,0:T(8,128)S(1)}, u32[]{:S(2)}, u32[]{:S(2)}) collective-permute-start(f32[1,8,64,128]{3,2,1,0:T(8,128)S(1)} %slice_select_fusion.own), channel_id=1, source_target_pairs={{1,3},{3,1},{17,19},{19,17},{2,6},{6,2},{18,22},{22,18},{7,5},{5,7... | collective-permute-start | bytes 786440 | tf_op jit(solution)/shard_map/ppermute | solution.py:338
  127.5 5.4 %collective-permute-start.12 = (f32[1,8,64,128]{3,2,1,0:T(8,128)S(1)}, f32[1,8,64,128]{3,2,1,0:T(8,128)S(1)}, u32[]{:S(2)}, u32[]{:S(2)}) collective-permute-start(f32[1,8,64,128]{3,2,1,0:T(8,128)S(1)} %slice_select_fusion.own), channel_id=1, source_target_pairs={{0,1},{1,0},{2,3},{3,2},{4,5},{5,4},{6,7},{7,6},{8,9},{9,8},{10,11... | collective-permute-start | bytes 786440 | tf_op jit(solution)/shard_map/ppermute | solution.py:338
  140.8 7.7 %collective-permute-start.15 = (f32[1,8,64,128]{3,2,1,0:T(8,128)S(1)}, f32[1,8,64,128]{3,2,1,0:T(8,128)S(1)}, u32[]{:S(2)}, u32[]{:S(2)}) collective-permute-start(f32[1,8,64,128]{3,2,1,0:T(8,128)S(1)} %get-tuple-element.26.own), channel_id=1, source_target_pairs={{1,3},{3,1},{17,19},{19,17},{2,6},{6,2},{18,22},{22,18},{7,5},{5,7... | collective-permute-start | bytes 786440 | tf_op jit(solution)/shard_map/ppermute | solution.py:338
  141.5 8.2 %collective-permute-start.14 = (f32[1,8,64,128]{3,2,1,0:T(8,128)S(1)}, f32[1,8,64,128]{3,2,1,0:T(8,128)S(1)}, u32[]{:S(2)}, u32[]{:S(2)}) collective-permute-start(f32[1,8,64,128]{3,2,1,0:T(8,128)S(1)} %get-tuple-element.26.own), channel_id=1, source_target_pairs={{0,1},{1,0},{2,3},{3,2},{4,5},{5,4},{6,7},{7,6},{8,9},{9,8},{10,11... | collective-permute-start | bytes 786440 | tf_op jit(solution)/shard_map/ppermute | solution.py:338
  159.7 40.8 %all-to-all-start.2 = ((f32[8,8,64,128]{3,2,1,0:T(8,128)}), f32[8,8,64,128]{3,2,1,0:T(8,128)S(1)}, u32[]{:S(2)}, u32[]{:S(2)}) async-start(f32[8,8,64,128]{3,2,1,0:T(8,128)} %copy-done.1), calls=%async_computation.2 | async-start | bytes 4194304 | tf_op jit(solution)/shard_map/all_to_all | solution.py:349
  200.5 2.7 %collective-permute-start.16 = (f32[4,8,64,128]{3,2,1,0:T(8,128)S(1)}, f32[4,8,64,128]{3,2,1,0:T(8,128)S(1)}, u32[]{:S(2)}, u32[]{:S(2)}) collective-permute-start(f32[4,8,64,128]{3,2,1,0:T(8,128)S(1)} %constant_dynamic-slice_fusion), channel_id=1, source_target_pairs={{0,1},{1,0},{2,3},{3,2},{4,5},{5,4},{6,7},{7,6},{8,9},{9,8},{10,11... | collective-permute-start | bytes 3145736 | tf_op jit(solution)/shard_map/ppermute | solution.py:406
  (1 other events, 1.3 us)

commit v4 on v3

--- a/solution.py
+++ b/solution.py
@@ -14,7 +14,7 @@
 LANES = 128
 ROWS = 8
 FILL = 4
-BATCH = 24
+BATCH = 16
 VMEM = 24 << 20
 
 
@@ -87,7 +87,7 @@
     return i ^ (i >> 1)
 
 
-def call(kernel, out_shape, operands, flags, scratch=(), flops=0, part=None):
+def call(kernel, out_shape, operands, flags, scratch=(), flops=0, part=None, grant=VMEM):
     specs = [pl.BlockSpec(memory_space=pltpu.VMEM)] * len(operands)
     grid = ()
     if part:
@@ -105,7 +105,7 @@
         out_specs=jax.tree.map(lambda _: pl.BlockSpec(memory_space=pltpu.VMEM), out_shape),
         scratch_shapes=list(scratch),
         cost_estimate=pl.CostEstimate(flops=flops or size, bytes_accessed=size, transcendentals=0),
-        compiler_params=pltpu.CompilerParams(vmem_limit_bytes=VMEM),
+        compiler_params=pltpu.CompilerParams(vmem_limit_bytes=grant),
     )(flags, *operands)
 
 
@@ -118,7 +118,7 @@
 
 
 def unrolled(count, one):
-    depth = math.gcd(count, 4)
+    depth = math.gcd(count, 8)
 
     def step(k, carry):
         for j in range(depth):
@@ -286,7 +286,7 @@
                 dst[1 + i, at : at + ROWS] = new
         dst[ghost, inside] = swap_lanes(dst[planes, inside])
 
-    def advance(first, step, carry):
+    def advance(first, step):
         def put_source(i, plane):
             c[i] = coef[2, i] * (va[1 + i, inside] + plane)
 
@@ -302,11 +302,9 @@
             low = region.tiles(va[1 + 2 * ROWS + m, inside])
             high = region.tiles(va[planes - m, inside])
             out[done + step, m] = jnp.where(region.left, low, high).reshape(-1, LANES)
-        return carry
-
-    half = steps // 2
-    lax.fori_loop(0, half, functools.partial(advance, 1), 0)
-    lax.fori_loop(half, steps, functools.partial(advance, SWEEPS * half + 1), 0)
+
+    for step in range(steps):
+        advance(SWEEPS * step + 1, step)
     last[0] = out[done + steps - 1]
 
 
@@ -340,7 +338,13 @@
     def packed(raw):
         zr = raw.shape[0]
         shapes = [jax.ShapeDtypeStruct((n * ROWS * zr, LANES), f32) for n in (blocks, blocks // 2)]
-        whole, send = call(functools.partial(format_kernel, blocks), shapes, (raw,), flags)
+        whole, send = call(
+            functools.partial(format_kernel, blocks),
+            shapes,
+            (raw,),
+            flags,
+            grant=None if zr == zlen else VMEM,
+        )
         got = lax.ppermute(send, "space", cores)
         whole = lax.dynamic_update_slice_in_dim(whole, got, (1 - s) * got.shape[0], 0)
         return whole.reshape(chips, ROWS, zr, LANES)

time: 208 us -> 204 us (0.981)
  local copies, waits for them, and re-layouts: 6.81 us -> 3.65 us
    unnamed x12 -> x10, local copies, waits for them, and re-layouts: 4.23 us -> 1.33 us
where the time goes in v4:
time: 204 us; the launch traced here: 203 us
  waiting for transfers between devices  68.1 us (33%)
  starting transfers between devices  63.2 us (31%)
  Pallas kernels  44 us (22%)
  blocking collectives  23.3 us (11%)
  local copies, waits for them, and re-layouts  3.65 us (2%)
    pallas_call x9, Pallas kernels, call(): pl.pallas_call(kernel, grid=grid, out_shape=out_shape, in_specs=[pl.Block...  44 us
    ppermute x12, starting transfers between devices, exchange(): return (lax.ppermute(x, 'space', cores), lax.ppermute(x, both, across))  36.3 us
    ppermute x1, waiting for transfers between devices, split_along_y(): lax.ppermute(fields, 'tm', [(i, (i + chips) % (2 * chips)) for i in range...  28.8 us
    all_to_all x2, waiting for transfers between devices, to_chips(): return lax.all_to_all(x, 'tm', 0, 0, axis_index_groups=groups, tiled=True)  24.6 us
    all_to_all x1, blocking collectives, to_chips(): return lax.all_to_all(x, 'tm', 0, 0, axis_index_groups=groups, tiled=True)  23.3 us
    all_to_all x2, starting transfers between devices, to_chips(): return lax.all_to_all(x, 'tm', 0, 0, axis_index_groups=groups, tiled=True)  22.3 us
    ppermute x2, waiting for transfers between devices, packed(): got = lax.ppermute(send, 'space', cores)  4.33 us
    ppermute x1, waiting for transfers between devices, split_along_y(): state = jnp.where(lower, fields[0:1], lax.ppermute(state, both, hop))  4.19 us
  transfers between devices with their start and end apart: 19, of which 9 were waited for; matrix products, arithmetic and copies ran while one was open for 1% of the time, Pallas kernels for 5%

profile of v4, /device:TPU:0, one launch (start us, length us, event | category | flops | bytes accessed | tf_op | source)
XLA Modules:
  0.0 203.3 jit_solution(11295307125085405839)
XLA Ops:
  0.6 5.4 %shard_map.47 = (f32[4096,128]{1,0:T(8,128)}, f32[2048,128]{1,0:T(8,128)}) custom-call(s32[3]{0:T(128)} %pad_add_fusion.flags, f32[64,64,128]{2,1,0:T(8,128)} %bitcast.20), custom_call_target="tpu_custom_call" | custom-call | flops 5242880 | bytes 5242880 | tf_op jit(solution)/shard_map/pallas_call | solution.py:100
  6.4 2.5 %collective-permute-done.2 = f32[2048,128]{1,0:T(8,128)S(1)} collective-permute-done((f32[2048,128]{1,0:T(8,128)}, f32[2048,128]{1,0:T(8,128)S(1)}, u32[]{:S(2)}, u32[]{:S(2)}) %collective-permute-start.2) | collective-permute-done | bytes 1048608 | tf_op jit(solution)/shard_map/ppermute | solution.py:348
  10.0 6.3 %all-to-all-start = ((f32[8,8,64,128]{3,2,1,0:T(8,128)}), f32[8,8,64,128]{3,2,1,0:T(8,128)S(1)}, u32[]{:S(2)}, u32[]{:S(2)}) async-start(f32[8,8,64,128]{3,2,1,0:T(8,128)} %bitcast.21), calls=%async_computation | async-start | bytes 4194304 | tf_op jit(solution)/shard_map/all_to_all | solution.py:353
  16.3 2.7 %collective-permute-start = (f32[3,4,64,128]{3,2,1,0:T(8,128)S(1)}, f32[3,4,64,128]{3,2,1,0:T(8,128)S(1)}, u32[]{:S(2)}, u32[]{:S(2)}) collective-permute-start(f32[3,4,64,128]{3,2,1,0:T(8,128)S(1)} %pad_maximum_fusion.1), channel_id=1, source_target_pairs={{0,16},{2,18},{4,20},{6,22},{8,24},{10,26},{12,28},{14,30},{16,0},... | collective-permute-start | bytes 1179656 | tf_op jit(solution)/shard_map/ppermute | solution.py:356
  19.0 28.8 %collective-permute-done = f32[3,4,64,128]{3,2,1,0:T(8,128)S(1)} collective-permute-done((f32[3,4,64,128]{3,2,1,0:T(8,128)S(1)}, f32[3,4,64,128]{3,2,1,0:T(8,128)S(1)}, u32[]{:S(2)}, u32[]{:S(2)}) %collective-permute-start) | collective-permute-done | bytes 393248 | tf_op jit(solution)/shard_map/ppermute | solution.py:356
  47.9 1.3 shard_map.46
  49.4 1.8 collective-permute-done.1
  52.2 23.3 %all_to_all.15.got = f32[8,8,24,128]{3,2,1,0:T(8,128)S(1)} all-to-all(f32[8,8,24,128]{3,2,1,0:T(8,128)S(1)} %bitcast.19), channel_id=1, replica_groups={{0,2,4,6,8,10,12,14},{16,18,20,22,24,26,28,30},{1,3,5,7,9,11,13,15},{17..., dimensions={0} | all-to-all | bytes 1572864 | tf_op jit(solution)/shard_map/all_to_all | solution.py:353
  77.9 2.4 %collective-permute-start.5 = (f32[4,8,64,128]{3,2,1,0:T(8,128)S(1)}, f32[4,8,64,128]{3,2,1,0:T(8,128)S(1)}, u32[]{:S(2)}, u32[]{:S(2)}) collective-permute-start(f32[4,8,64,128]{3,2,1,0:T(8,128)S(1)} %get-tuple-element.30), channel_id=1, source_target_pairs={{0,1},{1,0},{2,3},{3,2},{4,5},{5,4},{6,7},{7,6},{8,9},{9,8},{10,11... | collective-permute-start | bytes 3145736 | tf_op jit(solution)/shard_map/ppermute | solution.py:336
  81.1 6.4 %collective-permute-start.9 = (f32[4,8,64,128]{3,2,1,0:T(8,128)S(1)}, f32[4,8,64,128]{3,2,1,0:T(8,128)S(1)}, u32[]{:S(2)}, u32[]{:S(2)}) collective-permute-start(f32[4,8,64,128]{3,2,1,0:T(8,128)S(1)} %get-tuple-element.29), channel_id=1, source_target_pairs={{0,1},{1,0},{2,3},{3,2},{4,5},{5,4},{6,7},{7,6},{8,9},{9,8},{10,11... | collective-permute-start | bytes 3145736 | tf_op jit(solution)/shard_map/ppermute | solution.py:336
  88.8 7.3 %shard_map.50 = (f32[4,8,64,128]{3,2,1,0:T(8,128)S(1)}, f32[1,8,64,128]{3,2,1,0:T(8,128)S(1)}) custom-call(s32[3]{0:T(128)S(1)} %copy-done.1, f32[3,8,64,128]{3,2,1,0:T(8,128)S(1)} %shard_map.48.own, f32[3,8,64,128]{3,2,1,0:T(8,128)S(1)} %collective-permute-done.3.core, f32[3,8,64,128]{3,2,1,0:T(8,128)S(1)} %collective-permute-done.4.link, ...), custom_call_target="tpu_custom_call" | custom-call | flops 20971520 | bytes 10223616 | tf_op jit(solution)/shard_map/pallas_call | solution.py:100
  96.8 11.8 %collective-permute-start.7 = (f32[1,8,64,128]{3,2,1,0:T(8,128)S(1)}, f32[1,8,64,128]{3,2,1,0:T(8,128)S(1)}, u32[]{:S(2)}, u32[]{:S(2)}) collective-permute-start(f32[1,8,64,128]{3,2,1,0:T(8,128)S(1)} %get-tuple-element.23.own), channel_id=1, source_target_pairs={{0,1},{1,0},{2,3},{3,2},{4,5},{5,4},{6,7},{7,6},{8,9},{9,8},{10,11... | collective-permute-start | bytes 786440 | tf_op jit(solution)/shard_map/ppermute | solution.py:336
  109.8 8.7 %shard_map.51 = (f32[8,8,64,128]{3,2,1,0:T(8,128)}, f32[1,8,64,128]{3,2,1,0:T(8,128)S(1)}) custom-call(s32[3]{0:T(128)S(1)} %copy-done.1, f32[1,8,64,128]{3,2,1,0:T(8,128)S(1)} %get-tuple-element.23.own, f32[1,8,64,128]{3,2,1,0:T(8,128)S(1)} %collective-permute-done.7.core, f32[1,8,64,128]{3,2,1,0:T(8,128)S(1)} %collective-permute-done.8.link, ...), custom_call_target="tpu_custom_call" | custom-call | flops 20971520 | bytes 10747904 | tf_op jit(solution)/shard_map/pallas_call | solution.py:100
  118.4 1.5 collective-permute-start.11
  119.9 4.2 %collective-permute-done.11 = f32[1,8,64,128]{3,2,1,0:T(8,128)S(1)} collective-permute-done((f32[1,8,64,128]{3,2,1,0:T(8,128)S(1)}, f32[1,8,64,128]{3,2,1,0:T(8,128)S(1)}, u32[]{:S(2)}, u32[]{:S(2)}) %collective-permute-start.11) | collective-permute-done | bytes 262176 | tf_op jit(solution)/shard_map/ppermute | solution.py:406
  125.0 4.2 %collective-permute-start.12 = (f32[1,8,64,128]{3,2,1,0:T(8,128)S(1)}, f32[1,8,64,128]{3,2,1,0:T(8,128)S(1)}, u32[]{:S(2)}, u32[]{:S(2)}) collective-permute-start(f32[1,8,64,128]{3,2,1,0:T(8,128)S(1)} %slice_select_fusion.own), channel_id=1, source_target_pairs={{0,1},{1,0},{2,3},{3,2},{4,5},{5,4},{6,7},{7,6},{8,9},{9,8},{10,11... | collective-permute-start | bytes 786440 | tf_op jit(solution)/shard_map/ppermute | solution.py:336
  130.4 7.3 %shard_map.52 = (f32[4,8,64,128]{3,2,1,0:T(8,128)S(1)}, f32[1,8,64,128]{3,2,1,0:T(8,128)S(1)}) custom-call(s32[3]{0:T(128)S(1)} %copy-done.1, f32[1,8,64,128]{3,2,1,0:T(8,128)S(1)} %slice_select_fusion.own, f32[1,8,64,128]{3,2,1,0:T(8,128)S(1)} %collective-permute-done.12.core, f32[1,8,64,128]{3,2,1,0:T(8,128)S(1)} %collective-permute-done.13.link, ...), custom_call_target="tpu_custom_call" | custom-call | flops 20971520 | bytes 8650752 | tf_op jit(solution)/shard_map/pallas_call | solution.py:100
  138.3 7.0 %collective-permute-start.14 = (f32[1,8,64,128]{3,2,1,0:T(8,128)S(1)}, f32[1,8,64,128]{3,2,1,0:T(8,128)S(1)}, u32[]{:S(2)}, u32[]{:S(2)}) collective-permute-start(f32[1,8,64,128]{3,2,1,0:T(8,128)S(1)} %get-tuple-element.26.own), channel_id=1, source_target_pairs={{0,1},{1,0},{2,3},{3,2},{4,5},{5,4},{6,7},{7,6},{8,9},{9,8},{10,11... | collective-permute-start | bytes 786440 | tf_op jit(solution)/shard_map/ppermute | solution.py:336
  146.5 8.1 %shard_map.53 = (f32[8,8,64,128]{3,2,1,0:T(8,128)S(1)}, f32[1,8,64,128]{3,2,1,0:T(8,128)}) custom-call(s32[3]{0:T(128)S(1)} %copy-done.1, f32[1,8,64,128]{3,2,1,0:T(8,128)S(1)} %get-tuple-element.26.own, f32[1,8,64,128]{3,2,1,0:T(8,128)S(1)} %collective-permute-done.14.core, f32[1,8,64,128]{3,2,1,0:T(8,128)S(1)} %collective-permute-done.15.link, ...), custom_call_target="tpu_custom_call" | custom-call | flops 20971520 | bytes 10747904 | tf_op jit(solution)/shard_map/pallas_call | solution.py:100
  154.6 1.3 copy-done
  155.9 16.0 %all-to-all-start.2 = ((f32[8,8,64,128]{3,2,1,0:T(8,128)}), f32[8,8,64,128]{3,2,1,0:T(8,128)S(1)}, u32[]{:S(2)}, u32[]{:S(2)}) async-start(f32[8,8,64,128]{3,2,1,0:T(8,128)} %copy-done), calls=%async_computation.2 | async-start | bytes 4194304 | tf_op jit(solution)/shard_map/all_to_all | solution.py:353
  171.9 24.6 %all-to-all-done.2 = f32[8,8,64,128]{3,2,1,0:T(8,128)S(1)} async-done(((f32[8,8,64,128]{3,2,1,0:T(8,128)}), f32[8,8,64,128]{3,2,1,0:T(8,128)S(1)}, u32[]{:S(2)}, u32[]{:S(2)}) %all-to-all-start.2) | async-done | bytes 2097184 | tf_op jit(solution)/shard_map/all_to_all | solution.py:353
  196.7 2.6 %collective-permute-done.16 = f32[4,8,64,128]{3,2,1,0:T(8,128)S(1)} collective-permute-done((f32[4,8,64,128]{3,2,1,0:T(8,128)S(1)}, f32[4,8,64,128]{3,2,1,0:T(8,128)S(1)}, u32[]{:S(2)}, u32[]{:S(2)}) %collective-permute-start.16) | collective-permute-done | bytes 1048608 | tf_op jit(solution)/shard_map/ppermute | solution.py:410
  199.3 4.0 %shard_map.54 = f32[64,64,128]{2,1,0:T(8,128)} custom-call(s32[3]{0:T(128)S(1)} %copy-done.1, f32[4096,128]{1,0:T(8,128)S(1)} %bitcast.16, f32[2048,128]{1,0:T(8,128)S(1)} %bitcast.18), custom_call_target="tpu_custom_call" | custom-call | flops 5242880 | bytes 5242880 | tf_op jit(solution)/shard_map/pallas_call | solution.py:100
  (44 shorter events, 13.7 us)
Async XLA Ops:
  6.0 2.9 %collective-permute-start.2 = (f32[2048,128]{1,0:T(8,128)}, f32[2048,128]{1,0:T(8,128)S(1)}, u32[]{:S(2)}, u32[]{:S(2)}) collective-permute-start(f32[2048,128]{1,0:T(8,128)} %get-tuple-element.20), channel_id=1, source_target_pairs={{0,1},{1,0},{2,3},{3,2},{4,5},{5,4},{6,7},{7,6},{8,9},{9,8},{10,11... | collective-permute-start | bytes 3145736 | tf_op jit(solution)/shard_map/ppermute | solution.py:348
  9.9 6.3 %copy-start.2 = (f32[4,64,128]{2,1,0:T(8,128)S(1)}, f32[4,64,128]{2,1,0:T(8,128)}, u32[]{:S(2)}) copy-start(f32[4,64,128]{2,1,0:T(8,128)} %param.7) | copy-start | bytes 393220
  9.9 6.3 %copy-start.3 = (f32[4,64,128]{2,1,0:T(8,128)S(1)}, f32[4,64,128]{2,1,0:T(8,128)}, u32[]{:S(2)}) copy-start(f32[4,64,128]{2,1,0:T(8,128)} %param.6) | copy-start | bytes 393220
  10.0 6.3 %copy-start.4 = (f32[4,64,128]{2,1,0:T(8,128)S(1)}, f32[4,64,128]{2,1,0:T(8,128)}, u32[]{:S(2)}) copy-start(f32[4,64,128]{2,1,0:T(8,128)} %param.5) | copy-start | bytes 393220
  10.0 42.3 %all-to-all-start = ((f32[8,8,64,128]{3,2,1,0:T(8,128)}), f32[8,8,64,128]{3,2,1,0:T(8,128)S(1)}, u32[]{:S(2)}, u32[]{:S(2)}) async-start(f32[8,8,64,128]{3,2,1,0:T(8,128)} %bitcast.21), calls=%async_computation | async-start | bytes 4194304 | tf_op jit(solution)/shard_map/all_to_all | solution.py:353
  16.3 31.4 %collective-permute-start = (f32[3,4,64,128]{3,2,1,0:T(8,128)S(1)}, f32[3,4,64,128]{3,2,1,0:T(8,128)S(1)}, u32[]{:S(2)}, u32[]{:S(2)}) collective-permute-start(f32[3,4,64,128]{3,2,1,0:T(8,128)S(1)} %pad_maximum_fusion.1), channel_id=1, source_target_pairs={{0,16},{2,18},{4,20},{6,22},{8,24},{10,26},{12,28},{14,30},{16,0},... | collective-permute-start | bytes 1179656 | tf_op jit(solution)/shard_map/ppermute | solution.py:356
  18.9 29.0 %copy-start.1 = (s32[3]{0:T(128)S(1)}, s32[3]{0:T(128)}, u32[]{:S(2)}) copy-start(s32[3]{0:T(128)} %pad_add_fusion.flags) | copy-start | bytes 40
  49.3 1.9 collective-permute-start.1
  76.3 4.8 %collective-permute-start.4 = (f32[3,8,64,128]{3,2,1,0:T(8,128)S(1)}, f32[3,8,64,128]{3,2,1,0:T(8,128)S(1)}, u32[]{:S(2)}, u32[]{:S(2)}) collective-permute-start(f32[3,8,64,128]{3,2,1,0:T(8,128)S(1)} %shard_map.48.own), channel_id=1, source_target_pairs={{1,3},{3,1},{17,19},{19,17},{2,6},{6,2},{18,22},{22,18},{7,5},{5,7... | collective-permute-start | bytes 2359304 | tf_op jit(solution)/shard_map/ppermute | solution.py:336
  77.1 11.6 %collective-permute-start.6 = (f32[4,8,64,128]{3,2,1,0:T(8,128)S(1)}, f32[4,8,64,128]{3,2,1,0:T(8,128)S(1)}, u32[]{:S(2)}, u32[]{:S(2)}) collective-permute-start(f32[4,8,64,128]{3,2,1,0:T(8,128)S(1)} %get-tuple-element.30), channel_id=1, source_target_pairs={{1,3},{3,1},{17,19},{19,17},{2,6},{6,2},{18,22},{22,18},{7,5},{5,7... | collective-permute-start | bytes 3145736 | tf_op jit(solution)/shard_map/ppermute | solution.py:336
  77.9 10.9 %collective-permute-start.5 = (f32[4,8,64,128]{3,2,1,0:T(8,128)S(1)}, f32[4,8,64,128]{3,2,1,0:T(8,128)S(1)}, u32[]{:S(2)}, u32[]{:S(2)}) collective-permute-start(f32[4,8,64,128]{3,2,1,0:T(8,128)S(1)} %get-tuple-element.30), channel_id=1, source_target_pairs={{0,1},{1,0},{2,3},{3,2},{4,5},{5,4},{6,7},{7,6},{8,9},{9,8},{10,11... | collective-permute-start | bytes 3145736 | tf_op jit(solution)/shard_map/ppermute | solution.py:336
  80.3 7.2 %collective-permute-start.3 = (f32[3,8,64,128]{3,2,1,0:T(8,128)S(1)}, f32[3,8,64,128]{3,2,1,0:T(8,128)S(1)}, u32[]{:S(2)}, u32[]{:S(2)}) collective-permute-start(f32[3,8,64,128]{3,2,1,0:T(8,128)S(1)} %shard_map.48.own), channel_id=1, source_target_pairs={{0,1},{1,0},{2,3},{3,2},{4,5},{5,4},{6,7},{7,6},{8,9},{9,8},{10,11... | collective-permute-start | bytes 2359304 | tf_op jit(solution)/shard_map/ppermute | solution.py:336
  80.3 28.3 %collective-permute-start.10 = (f32[4,8,64,128]{3,2,1,0:T(8,128)S(1)}, f32[4,8,64,128]{3,2,1,0:T(8,128)S(1)}, u32[]{:S(2)}, u32[]{:S(2)}) collective-permute-start(f32[4,8,64,128]{3,2,1,0:T(8,128)S(1)} %get-tuple-element.29), channel_id=1, source_target_pairs={{1,3},{3,1},{17,19},{19,17},{2,6},{6,2},{18,22},{22,18},{7,5},{5,7... | collective-permute-start | bytes 3145736 | tf_op jit(solution)/shard_map/ppermute | solution.py:336
  81.1 27.5 %collective-permute-start.9 = (f32[4,8,64,128]{3,2,1,0:T(8,128)S(1)}, f32[4,8,64,128]{3,2,1,0:T(8,128)S(1)}, u32[]{:S(2)}, u32[]{:S(2)}) collective-permute-start(f32[4,8,64,128]{3,2,1,0:T(8,128)S(1)} %get-tuple-element.29), channel_id=1, source_target_pairs={{0,1},{1,0},{2,3},{3,2},{4,5},{5,4},{6,7},{7,6},{8,9},{9,8},{10,11... | collective-permute-start | bytes 3145736 | tf_op jit(solution)/shard_map/ppermute | solution.py:336
  96.1 12.5 %collective-permute-start.8 = (f32[1,8,64,128]{3,2,1,0:T(8,128)S(1)}, f32[1,8,64,128]{3,2,1,0:T(8,128)S(1)}, u32[]{:S(2)}, u32[]{:S(2)}) collective-permute-start(f32[1,8,64,128]{3,2,1,0:T(8,128)S(1)} %get-tuple-element.23.own), channel_id=1, source_target_pairs={{1,3},{3,1},{17,19},{19,17},{2,6},{6,2},{18,22},{22,18},{7,5},{5,7... | collective-permute-start | bytes 786440 | tf_op jit(solution)/shard_map/ppermute | solution.py:336
  96.8 13.0 %collective-permute-start.7 = (f32[1,8,64,128]{3,2,1,0:T(8,128)S(1)}, f32[1,8,64,128]{3,2,1,0:T(8,128)S(1)}, u32[]{:S(2)}, u32[]{:S(2)}) collective-permute-start(f32[1,8,64,128]{3,2,1,0:T(8,128)S(1)} %get-tuple-element.23.own), channel_id=1, source_target_pairs={{0,1},{1,0},{2,3},{3,2},{4,5},{5,4},{6,7},{7,6},{8,9},{9,8},{10,11... | collective-permute-start | bytes 786440 | tf_op jit(solution)/shard_map/ppermute | solution.py:336
  118.4 5.6 %collective-permute-start.11 = (f32[1,8,64,128]{3,2,1,0:T(8,128)S(1)}, f32[1,8,64,128]{3,2,1,0:T(8,128)S(1)}, u32[]{:S(2)}, u32[]{:S(2)}) collective-permute-start(f32[1,8,64,128]{3,2,1,0:T(8,128)S(1)} %get-tuple-element.25), channel_id=1, source_target_pairs={{0,16},{1,17},{2,18},{3,19},{4,20},{5,21},{6,22},{7,23},{8,24},{9,... | collective-permute-start | bytes 786440 | tf_op jit(solution)/shard_map/ppermute | solution.py:406
  124.1 5.1 %collective-permute-start.13 = (f32[1,8,64,128]{3,2,1,0:T(8,128)S(1)}, f32[1,8,64,128]{3,2,1,0:T(8,128)S(1)}, u32[]{:S(2)}, u32[]{:S(2)}) collective-permute-start(f32[1,8,64,128]{3,2,1,0:T(8,128)S(1)} %slice_select_fusion.own), channel_id=1, source_target_pairs={{1,3},{3,1},{17,19},{19,17},{2,6},{6,2},{18,22},{22,18},{7,5},{5,7... | collective-permute-start | bytes 786440 | tf_op jit(solution)/shard_map/ppermute | solution.py:336
  125.0 5.4 %collective-permute-start.12 = (f32[1,8,64,128]{3,2,1,0:T(8,128)S(1)}, f32[1,8,64,128]{3,2,1,0:T(8,128)S(1)}, u32[]{:S(2)}, u32[]{:S(2)}) collective-permute-start(f32[1,8,64,128]{3,2,1,0:T(8,128)S(1)} %slice_select_fusion.own), channel_id=1, source_target_pairs={{0,1},{1,0},{2,3},{3,2},{4,5},{5,4},{6,7},{7,6},{8,9},{9,8},{10,11... | collective-permute-start | bytes 786440 | tf_op jit(solution)/shard_map/ppermute | solution.py:336
  137.7 7.7 %collective-permute-start.15 = (f32[1,8,64,128]{3,2,1,0:T(8,128)S(1)}, f32[1,8,64,128]{3,2,1,0:T(8,128)S(1)}, u32[]{:S(2)}, u32[]{:S(2)}) collective-permute-start(f32[1,8,64,128]{3,2,1,0:T(8,128)S(1)} %get-tuple-element.26.own), channel_id=1, source_target_pairs={{1,3},{3,1},{17,19},{19,17},{2,6},{6,2},{18,22},{22,18},{7,5},{5,7... | collective-permute-start | bytes 786440 | tf_op jit(solution)/shard_map/ppermute | solution.py:336
  138.3 8.2 %collective-permute-start.14 = (f32[1,8,64,128]{3,2,1,0:T(8,128)S(1)}, f32[1,8,64,128]{3,2,1,0:T(8,128)S(1)}, u32[]{:S(2)}, u32[]{:S(2)}) collective-permute-start(f32[1,8,64,128]{3,2,1,0:T(8,128)S(1)} %get-tuple-element.26.own), channel_id=1, source_target_pairs={{0,1},{1,0},{2,3},{3,2},{4,5},{5,4},{6,7},{7,6},{8,9},{9,8},{10,11... | collective-permute-start | bytes 786440 | tf_op jit(solution)/shard_map/ppermute | solution.py:336
  154.6 1.3 copy-start
  155.9 40.6 %all-to-all-start.2 = ((f32[8,8,64,128]{3,2,1,0:T(8,128)}), f32[8,8,64,128]{3,2,1,0:T(8,128)S(1)}, u32[]{:S(2)}, u32[]{:S(2)}) async-start(f32[8,8,64,128]{3,2,1,0:T(8,128)} %copy-done), calls=%async_computation.2 | async-start | bytes 4194304 | tf_op jit(solution)/shard_map/all_to_all | solution.py:353
  196.6 2.7 %collective-permute-start.16 = (f32[4,8,64,128]{3,2,1,0:T(8,128)S(1)}, f32[4,8,64,128]{3,2,1,0:T(8,128)S(1)}, u32[]{:S(2)}, u32[]{:S(2)}) collective-permute-start(f32[4,8,64,128]{3,2,1,0:T(8,128)S(1)} %constant_dynamic-slice_fusion), channel_id=1, source_target_pairs={{0,1},{1,0},{2,3},{3,2},{4,5},{5,4},{6,7},{7,6},{8,9},{9,8},{10,11... | collective-permute-start | bytes 3145736 | tf_op jit(solution)/shard_map/ppermute | solution.py:410
